TPU v7x, 32 devices: a whole 2x2x4 slice. The times are simulated.
32 devices in a mesh: ba: 8 (over z, core), ha: 4 (over y, x).
Axes of the slice: x: 2, y: 2, z: 4, core: 2. Of those that a mesh axis runs over, the one named last changes fastest.
Arguments:
- queries: bfloat16 [2048, 64, 576], P('ba', 'ha'), may hold values from -6 to 6
- out_grad: bfloat16 [2048, 64, 512], P('ba', 'ha'), may hold values from -1.1953125 to 1.1953125
- out_saved: bfloat16 [2048, 64, 512], P('ba', 'ha'), may hold values from -3 to 3
- logsumexp: float32 [2048, 64], P('ba', 'ha'), may hold values from 7 to 9
- parents: int32 [2048], P('ba'), may hold values from 0 to 511, as said below
- latents: bfloat16 [512, 576], P(('ba', 'ha')), may hold values from -6 to 6
- hidden: bfloat16 [512, 7168], P('ba', 'ha'), may hold values from -6 to 6
- latent_weight: bfloat16 [576, 7168], P(None, 'ha'), may hold values from -0.0625 to 0.0625
Outputs:
- query_grad: bfloat16 [2048, 64, 576], P('ba', 'ha')
- weight_grad: bfloat16 [576, 7168], P('ba', 'ha')
- input_grad: bfloat16 [512, 7168], P('ba', 'ha')
Inputs may be any that keep to these rules, and one draw needn't show every extreme that they name: `parents`: the 32 tokens of each aligned block of 32 share one value; some token has 0 and some has 511.
All inputs are finite; a program needn't handle non-finite values.
Results may differ from a plain program's by a relative error of at most 0.0067.
Values may be sent and summed in bfloat16 or wider, within the bound.
No kernel may reach another device: no remote copies, remote signals or barrier semaphores. Data moves between devices by JAX's collectives and lax.ppermute only.
A program may use at most 64 MiB of HBM per device.

v0:
```python
import jax
import jax.numpy as jnp
from jax import lax
from jax.sharding import PartitionSpec as P

RANK = 512
ROPE = 64


softmax_scale = 192.0 ** (-0.5)


def tile_terms(query_rows, grad_rows, lse_rows, deltas, limits, key_block, offset):
    key_count = key_block.shape[0]
    key_index = offset + jnp.arange(key_count, dtype=jnp.int32)
    scores = (
        jnp.einsum("qd,kd->qk", query_rows, key_block, preferred_element_type=jnp.float32)
        * softmax_scale
    )
    visible = key_index[None, :] <= limits[:, None]
    weights = jnp.where(visible, jnp.exp(scores - lse_rows[:, None]), jnp.float32(0.0))
    grad_prob = jnp.einsum(
        "qd,kd->qk", grad_rows, key_block[:, :RANK], preferred_element_type=jnp.float32
    )
    grad_score = (weights * (grad_prob - deltas[:, None])).astype(jnp.bfloat16)
    query_part = jnp.einsum("qk,kd->qd", grad_score, key_block, preferred_element_type=jnp.float32)
    value_part = jnp.einsum(
        "qk,qd->kd", weights.astype(jnp.bfloat16), grad_rows, preferred_element_type=jnp.float32
    )
    key_grad = softmax_scale * jnp.einsum(
        "qk,qd->kd", grad_score, query_rows, preferred_element_type=jnp.float32
    )
    key_grad = key_grad + jnp.pad(value_part, ((0, 0), (0, ROPE)))
    return (query_part, key_grad)


def on_device(queries, out_grad, out_saved, logsumexp, parents, latents, hidden, latent_weight):
    tokens_here, heads_here, full_width = queries.shape
    row_total = tokens_here * heads_here
    query_rows = queries.reshape(row_total, full_width)
    grad_rows = out_grad.reshape(row_total, RANK)
    saved_rows = out_saved.reshape(row_total, RANK)
    lse_rows = logsumexp.reshape(row_total)
    limits = jnp.repeat(parents, heads_here)
    deltas = jnp.sum(saved_rows.astype(jnp.float32) * grad_rows.astype(jnp.float32), axis=1)
    all_keys = lax.all_gather(latents, ("ba", "ha"), axis=0, tiled=True)
    prefix_total = all_keys.shape[0]
    tile_len = min(256, prefix_total)
    tile_count = prefix_total // tile_len
    key_tiles = all_keys.reshape(tile_count, tile_len, full_width)
    offsets = jnp.arange(tile_count, dtype=jnp.int32) * tile_len

    def tile_step(query_acc, tile_inputs):
        key_block, offset = tile_inputs
        query_part, key_grad = tile_terms(
            query_rows, grad_rows, lse_rows, deltas, limits, key_block, offset
        )
        return (query_acc + query_part, key_grad)

    query_acc, key_stack = lax.scan(
        tile_step, jnp.zeros((row_total, full_width), jnp.float32), (key_tiles, offsets)
    )
    latent_acc = key_stack.reshape(prefix_total, full_width)
    query_grad = (
        (softmax_scale * query_acc)
        .astype(jnp.bfloat16)
        .reshape(tokens_here, heads_here, full_width)
    )
    branch_part = lax.psum_scatter(latent_acc, "ba", scatter_dimension=0, tiled=True)
    row_grads = lax.psum(branch_part, "ha").astype(jnp.bfloat16)
    weight_grad = lax.psum_scatter(
        jnp.einsum("pl,ph->lh", row_grads, hidden, preferred_element_type=jnp.float32),
        "ba",
        scatter_dimension=0,
        tiled=True,
    ).astype(jnp.bfloat16)
    input_grad = jnp.dot(row_grads, latent_weight, preferred_element_type=jnp.float32).astype(
        jnp.bfloat16
    )
    return (query_grad, weight_grad, input_grad)


def solution(mesh):
    return jax.shard_map(
        on_device,
        mesh=mesh,
        in_specs=(
            P("ba", "ha", None),
            P("ba", "ha", None),
            P("ba", "ha", None),
            P("ba", "ha"),
            P("ba"),
            P(("ba", "ha"), None),
            P("ba", "ha"),
            P(None, "ha"),
        ),
        out_specs=(P("ba", "ha", None), P("ba", "ha"), P("ba", "ha")),
        check_vma=False,
    )
```

profile of v0, /device:TPU:0, one launch (start us, length us, event | category | flops | bytes accessed | tf_op | source)
XLA Modules:
  0.0 245.1 jit_solution(18365195262082448630)
XLA Ops:
  7.2 0.0 copy-start
  7.2 0.0 reduce-scatter.7.cloned.1.call-start
  7.3 0.9 copy.21
  8.2 0.1 sub.59
  8.3 0.0 copy-start.8
  8.3 4.6 %multiply_reduce_fusion = f32[256,16]{1,0:T(8,128)S(1)} fusion(bf16[256,16,512]{2,1,0:T(8,128)(2,1)} %param.11, bf16[256,16,512]{2,1,0:T(8,128)(2,1)} %param.12), kind=kLoop, calls=%fused_computation.21 | loop fusion | flops 8384512 | bytes 8404992 | tf_op jit(solution)/shard_map/reduce_sum | solution.py:45
  13.0 0.1 reduce_sum.12
  13.1 73.2 %all_gather.3 = bf16[512,576]{1,0:T(8,128)(2,1)S(1)} all-gather(bf16[16,576]{1,0:T(8,128)(2,1)S(1)} %copy-done.8), channel_id=1, replica_groups=mesh['ba'=8,'ha'=4] {'ba','ha'}, dimensions={0}, use_global_device_ids=true | all-gather | bytes 608256 | tf_op jit(solution)/shard_map/all_gather | solution.py:46
  86.3 9.0 %copy.20 = bf16[256,16,576]{2,1,0:T(8,128)(2,1)} copy(bf16[256,16,576]{0,2,1:T(8,128)(2,1)} %param.10) | data formatting | bytes 9437184 | tf_op args[0]
  95.2 36.9 %while.16 = (s32[]{:T(128)}, f32[4096,576]{0,1:T(8,128)}, f32[2,256,576]{1,2,0:T(8,128)}, s32[2]{0:T(128)S(1)}, bf16[2,256,576]{2,1,0:T(8,128)(2,1)S(1)}, /*inde...) while((s32[]{:T(128)}, f32[4096,576]{0,1:T(8,128)}, ...), condition=%wide.wide.region_2.3_spmd.clone, body=%wide.wide.region_1.2_spmd.clone.sunk | while | flops 5784764416 | bytes 167284112 | solution.py:60
  95.2 0.6 dynamic_slice.22
  95.8 0.6 iota_add_fusion.3
  96.5 0.1 broadcast_in_dim.40
  96.6 0.1 le.46
  96.7 0.0 copy-start.2
  96.7 0.0 slice-start.3
  96.7 4.6 %fusion.69 = f32[4096,256]{0,1:T(8,128)S(1)} fusion(bf16[256,576]{1,0:T(8,128)(2,1)S(1)} %dynamic-slice_bitcast_fusion.3, bf16[4096,576]{1,0:T(8,128)(2,1)} %get-tuple-element.351, f32[4096]{0:T(1024)S(1)} %get-tuple-element.356, s32[4096]{0:T(1024)S(1)} %le.46, s32[256]{0:T(256)S(1)} %iota_add_fusion.3), kind=kOutput, calls=%fused_computation.9.clone.clone.1 | convolution fusion | flops 1212153856 | bytes 9241600 | tf_op jit(solution)/shard_map/while/body/eval_jaxpr/qd,kd->qk/dot_general | solution.py:17
  101.4 0.0 slice-start.4
  101.4 1.8 fusion.71
  103.2 0.0 slice-start
  103.2 0.0 slice-start.1
  103.2 1.3 fusion.70
  104.6 0.0 slice-start.2
  104.6 2.1 fusion.72
  106.7 0.3 slice-done.1
  107.0 0.5 slice-done.2
  107.5 2.6 %select_add_fusion.3 = f32[4096,576]{0,1:T(8,128)S(1)} fusion(f32[4096,576]{0,1:T(8,128)S(1)} %bitcast.75, bf16[4096,256]{0,1:T(8,128)(2,1)S(1)} %fusion.70, bf16[256,576]{1,0:T(8,128)(2,1)S(1)} %dynamic-slice_bitcast_fusion.3, pred[]{:T(512)S(6)} %compare.5), kind=kOutput, calls=%fused_computation.1.clone.clone.1 | convolution fusion | flops 1212678144 | bytes 21266432 | tf_op jit(solution)/shard_map/while/body/eval_jaxpr/qk,kd->qd/dot_general | solution.py:26
  110.0 3.7 %copy-done.1 = f32[4096,576]{0,1:T(8,128)} copy-done((f32[4096,576]{0,1:T(8,128)}, f32[4096,576]{0,1:T(8,128)S(1)}, u32[]{:S(2)}) %copy-start.1) | copy-done | bytes 9437208 | tf_op jit(solution)/shard_map/while
  113.7 0.6 dynamic_slice.22
  114.3 0.6 iota_add_fusion.3
  114.9 0.1 broadcast_in_dim.40
  115.0 0.1 le.46
  115.2 0.0 copy-start.2
  115.2 0.0 slice-start.3
  115.2 4.6 %fusion.69 = f32[4096,256]{0,1:T(8,128)S(1)} fusion(bf16[256,576]{1,0:T(8,128)(2,1)S(1)} %dynamic-slice_bitcast_fusion.3, bf16[4096,576]{1,0:T(8,128)(2,1)} %get-tuple-element.351, f32[4096]{0:T(1024)S(1)} %get-tuple-element.356, s32[4096]{0:T(1024)S(1)} %le.46, s32[256]{0:T(256)S(1)} %iota_add_fusion.3), kind=kOutput, calls=%fused_computation.9.clone.clone.1 | convolution fusion | flops 1212153856 | bytes 9241600 | tf_op jit(solution)/shard_map/while/body/eval_jaxpr/qd,kd->qk/dot_general | solution.py:17
  119.8 0.0 copy-done.2
  119.8 0.0 slice-start.4
  119.8 1.8 fusion.71
  121.7 0.0 slice-start
  121.7 0.0 slice-start.1
  121.7 1.3 fusion.70
  123.0 0.0 slice-start.2
  123.0 2.1 fusion.72
  125.2 0.0 slice-done
  125.2 0.3 slice-done.1
  125.5 0.5 slice-done.2
  125.9 2.6 %select_add_fusion.3 = f32[4096,576]{0,1:T(8,128)S(1)} fusion(f32[4096,576]{0,1:T(8,128)S(1)} %bitcast.75, bf16[4096,256]{0,1:T(8,128)(2,1)S(1)} %fusion.70, bf16[256,576]{1,0:T(8,128)(2,1)S(1)} %dynamic-slice_bitcast_fusion.3, pred[]{:T(512)S(6)} %compare.5), kind=kOutput, calls=%fused_computation.1.clone.clone.1 | convolution fusion | flops 1212678144 | bytes 21266432 | tf_op jit(solution)/shard_map/while/body/eval_jaxpr/qk,kd->qd/dot_general | solution.py:26
  128.5 0.0 copy-done.4
  128.5 0.0 copy-start.1
  128.5 3.7 %copy-done.1 = f32[4096,576]{0,1:T(8,128)} copy-done((f32[4096,576]{0,1:T(8,128)}, f32[4096,576]{0,1:T(8,128)S(1)}, u32[]{:S(2)}) %copy-start.1) | copy-done | bytes 9437208 | tf_op jit(solution)/shard_map/while
  132.2 2.8 %copy.28 = f32[2,256,576]{2,1,0:T(8,128)} copy(f32[2,256,576]{1,2,0:T(8,128)} %get-tuple-element.130) | data formatting | bytes 2359296
  134.9 0.0 reduce-scatter.7.cloned.1.call-update
  135.0 0.2 reduce-scatter.5.cloned.1.call-start
  135.2 29.1 %reduce-scatter.7.cloned.1.call-done = f32[64,576]{1,0:T(8,128)} async-done(((f32[512,576]{1,0:T(8,128)}), f32[64,576]{1,0:T(8,128)}) %reduce-scatter.7.cloned.1.call-update) | async-done | bytes 147472
  164.3 1.1 copy.27
  165.3 20.5 %all-reduce.2 = bf16[64,576]{0,1:T(8,128)(2,1)S(1)} all-reduce(f32[64,576]{0,1:T(8,128)S(1)} %copy.27), channel_id=1, replica_groups=mesh['ba'=8,'ha'=4] {'ha'}, use_global_device_ids=true, to_apply=%region_4.5 | all-reduce | flops 36864 | bytes 221184 | tf_op jit(solution)/shard_map/psum | solution.py:70
  185.9 2.7 %fusion.18 = f32[576,1792]{1,0:T(8,128)} fusion(bf16[64,576]{0,1:T(8,128)(2,1)S(1)} %all-reduce.2, bf16[64,1792]{1,0:T(8,128)(2,1)S(1)} %copy-done.6), kind=kOutput, calls=%fused_computation.27 | convolution fusion | flops 132120576 | bytes 4431872 | tf_op jit(solution)/shard_map/pl,ph->lh/dot_general | solution.py:72
  188.6 0.0 reduce-scatter.5.cloned.1.call-update
  188.6 7.0 %multiply_convert_fusion = bf16[4096,576]{0,1:T(8,128)(2,1)} fusion(f32[4096,576]{0,1:T(8,128)} %get-tuple-element.129), kind=kLoop, calls=%fused_computation.20 | loop fusion | flops 4718592 | bytes 14155776 | tf_op jit(solution)/shard_map/convert_element_type | solution.py:66
  195.7 7.6 %copy.22 = bf16[4096,576]{1,0:T(8,128)(2,1)} copy(bf16[4096,576]{0,1:T(8,128)(2,1)} %multiply_convert_fusion) | data formatting | bytes 9437184 | tf_op jit(solution)/shard_map/convert_element_type | solution.py:66
  203.3 8.2 %copy.24 = bf16[256,16,576]{0,2,1:T(8,128)(2,1)} copy(bf16[256,16,576]{2,1,0:T(8,128)(2,1)} %bitcast.77) | data formatting | bytes 9437184
  211.5 1.2 convolution_convert_fusion
  212.8 23.7 %reduce-scatter.5.cloned.1.call-done = f32[72,1792]{1,0:T(8,128)} async-done(((f32[576,1792]{1,0:T(8,128)}), f32[72,1792]{1,0:T(8,128)}) %reduce-scatter.5.cloned.1.call-update) | async-done | bytes 516112 | tf_op jit(solution)/shard_map/reduce_scatter | solution.py:71
  236.5 1.8 convert_element_type.40
  (31 shorter events, 0.1 us)
Async XLA Ops:
  7.2 204.4 %copy-start = (bf16[576,1792]{1,0:T(8,128)(2,1)S(1)}, bf16[576,1792]{1,0:T(8,128)(2,1)}, u32[]{:S(2)}) copy-start(bf16[576,1792]{1,0:T(8,128)(2,1)} %param.17) | copy-start | bytes 6193156
  7.2 157.1 %reduce-scatter.7.cloned.1.call-start = ((), (), s32[]{:S(2)}) async-start(), calls=%async_computation.3 | async-start | bytes 1474560
  8.2 4.8 %copy-start.5 = (f32[256,16]{1,0:T(8,128)}, f32[256,16]{1,0:T(8,128)S(1)}, u32[]{:S(2)}) copy-start(f32[256,16]{1,0:T(8,128)S(1)} %copy.21) | copy-start | bytes 49156
  8.3 4.8 %copy-start.8 = (bf16[16,576]{1,0:T(8,128)(2,1)S(1)}, bf16[16,576]{1,0:T(8,128)(2,1)}, u32[]{:S(2)}) copy-start(bf16[16,576]{1,0:T(8,128)(2,1)} %param.15) | copy-start | bytes 55300
  86.3 9.0 %copy-start.7 = (s32[256]{0:T(256)S(1)}, s32[256]{0:T(256)}, u32[]{:S(2)}) copy-start(s32[256]{0:T(256)} %param.14) | copy-start | bytes 3076
  96.7 4.6 %copy-start.2 = (bf16[4096,512]{1,0:T(8,128)(2,1)S(1)}, bf16[4096,512]{1,0:T(8,128)(2,1)}, u32[]{:S(2)}) copy-start(bf16[4096,512]{1,0:T(8,128)(2,1)} %get-tuple-element.353) | copy-start | bytes 12582916 | tf_op jit(solution)/shard_map/while
  96.7 7.8 %slice-start.3 = ((s8[5242880]{0:T(1024)(128)(4,1)}), s8[4194304]{0:T(1024)(128)(4,1)S(1)}, s32[]{:S(2)}) async-start(s8[5242880]{0:T(1024)(128)(4,1)} %bitcast.80), calls=%async_computation.7 | async-start | bytes 8388608 | tf_op jit(solution)/shard_map/while
  101.4 3.2 %slice-start.4 = ((s8[5242880]{0:T(1024)(128)(4,1)}), s8[1048576]{0:T(1024)(128)(4,1)S(1)}, s32[]{:S(2)}) async-start(s8[5242880]{0:T(1024)(128)(4,1)} %bitcast.80), calls=%async_computation.8 | async-start | bytes 2097152 | tf_op jit(solution)/shard_map/while
  103.2 1.4 copy-start.3
  103.2 3.5 %slice-start = ((s8[9437184]{0:T(1024)(128)(4,1)}), s8[4194304]{0:T(1024)(128)(4,1)S(1)}, s32[]{:S(2)}) async-start(s8[9437184]{0:T(1024)(128)(4,1)} %bitcast.74), calls=%async_computation.4 | async-start | bytes 8388608 | tf_op jit(solution)/shard_map/while
  103.2 3.8 %slice-start.1 = ((s8[9437184]{0:T(1024)(128)(4,1)}), s8[4194304]{0:T(1024)(128)(4,1)S(1)}, s32[]{:S(2)}) async-start(s8[9437184]{0:T(1024)(128)(4,1)} %bitcast.74), calls=%async_computation.5 | async-start | bytes 8388608 | tf_op jit(solution)/shard_map/while
  104.6 2.9 %slice-start.2 = ((s8[9437184]{0:T(1024)(128)(4,1)}), s8[1048576]{0:T(1024)(128)(4,1)S(1)}, s32[]{:S(2)}) async-start(s8[9437184]{0:T(1024)(128)(4,1)} %bitcast.74), calls=%async_computation.6 | async-start | bytes 2097152 | tf_op jit(solution)/shard_map/while
  107.5 2.6 %copy-start.4 = (f32[2,256,576]{1,2,0:T(8,128)}, f32[2,256,576]{1,2,0:T(8,128)S(1)}, u32[]{:S(2)}) copy-start(f32[2,256,576]{1,2,0:T(8,128)S(1)} %fusion.72) | copy-start | bytes 3538948 | tf_op jit(solution)/shard_map/while
  110.0 3.7 %copy-start.1 = (f32[4096,576]{0,1:T(8,128)}, f32[4096,576]{0,1:T(8,128)S(1)}, u32[]{:S(2)}) copy-start(f32[4096,576]{0,1:T(8,128)S(1)} %select_add_fusion.3) | copy-start | bytes 28311556 | tf_op jit(solution)/shard_map/while
  115.2 4.6 %copy-start.2 = (bf16[4096,512]{1,0:T(8,128)(2,1)S(1)}, bf16[4096,512]{1,0:T(8,128)(2,1)}, u32[]{:S(2)}) copy-start(bf16[4096,512]{1,0:T(8,128)(2,1)} %get-tuple-element.353) | copy-start | bytes 12582916 | tf_op jit(solution)/shard_map/while
  115.2 7.8 %slice-start.3 = ((s8[5242880]{0:T(1024)(128)(4,1)}), s8[4194304]{0:T(1024)(128)(4,1)S(1)}, s32[]{:S(2)}) async-start(s8[5242880]{0:T(1024)(128)(4,1)} %bitcast.80), calls=%async_computation.7 | async-start | bytes 8388608 | tf_op jit(solution)/shard_map/while
  119.8 3.2 %slice-start.4 = ((s8[5242880]{0:T(1024)(128)(4,1)}), s8[1048576]{0:T(1024)(128)(4,1)S(1)}, s32[]{:S(2)}) async-start(s8[5242880]{0:T(1024)(128)(4,1)} %bitcast.80), calls=%async_computation.8 | async-start | bytes 2097152 | tf_op jit(solution)/shard_map/while
  121.7 1.4 copy-start.3
  121.7 3.5 %slice-start = ((s8[9437184]{0:T(1024)(128)(4,1)}), s8[4194304]{0:T(1024)(128)(4,1)S(1)}, s32[]{:S(2)}) async-start(s8[9437184]{0:T(1024)(128)(4,1)} %bitcast.74), calls=%async_computation.4 | async-start | bytes 8388608 | tf_op jit(solution)/shard_map/while
  121.7 3.8 %slice-start.1 = ((s8[9437184]{0:T(1024)(128)(4,1)}), s8[4194304]{0:T(1024)(128)(4,1)S(1)}, s32[]{:S(2)}) async-start(s8[9437184]{0:T(1024)(128)(4,1)} %bitcast.74), calls=%async_computation.5 | async-start | bytes 8388608 | tf_op jit(solution)/shard_map/while
  123.0 2.9 %slice-start.2 = ((s8[9437184]{0:T(1024)(128)(4,1)}), s8[1048576]{0:T(1024)(128)(4,1)S(1)}, s32[]{:S(2)}) async-start(s8[9437184]{0:T(1024)(128)(4,1)} %bitcast.74), calls=%async_computation.6 | async-start | bytes 2097152 | tf_op jit(solution)/shard_map/while
  125.9 2.6 %copy-start.4 = (f32[2,256,576]{1,2,0:T(8,128)}, f32[2,256,576]{1,2,0:T(8,128)S(1)}, u32[]{:S(2)}) copy-start(f32[2,256,576]{1,2,0:T(8,128)S(1)} %fusion.72) | copy-start | bytes 3538948 | tf_op jit(solution)/shard_map/while
  128.5 3.7 %copy-start.1 = (f32[4096,576]{0,1:T(8,128)}, f32[4096,576]{0,1:T(8,128)S(1)}, u32[]{:S(2)}) copy-start(f32[4096,576]{0,1:T(8,128)S(1)} %select_add_fusion.3) | copy-start | bytes 28311556 | tf_op jit(solution)/shard_map/while
  132.2 53.7 %copy-start.6 = (bf16[64,1792]{1,0:T(8,128)(2,1)S(1)}, bf16[64,1792]{1,0:T(8,128)(2,1)}, u32[]{:S(2)}) copy-start(bf16[64,1792]{1,0:T(8,128)(2,1)} %param.16) | copy-start | bytes 688132
  135.0 101.5 %reduce-scatter.5.cloned.1.call-start = ((), (), s32[]{:S(2)}) async-start(), calls=%async_computation.2 | async-start | bytes 4644864 | tf_op jit(solution)/shard_map/reduce_scatter | solution.py:71
Sparse Core Ops, SparseCore 0:
  135.1 29.1 reduce-scatter.6
  188.8 47.6 reduce-scatter.4
where the time goes:
time: 246 us; the launch traced here: 245 us
  blocking collectives  93.7 us (38%)
  waiting for transfers between devices  52.8 us (21%)
  local copies, waits for them, and re-layouts  40.3 us (16%)
  matrix products  28.7 us (12%)
  other arithmetic  14.7 us (6%)
  between operations  14.1 us (6%)
    all_gather x1, blocking collectives, on_device(): all_keys = lax.all_gather(latents, ('ba', 'ha'), axis=0, tiled=True)  73.2 us
    unnamed x3, waiting for transfers between devices  29.1 us
    reduce_scatter x1, waiting for transfers between devices, on_device(): lax.psum_scatter(jnp.einsum('pl,ph->lh', row_grads, hidden, preferred_ele...  23.7 us
    unnamed x15, local copies, waits for them, and re-layouts  22 us
    psum x1, blocking collectives, on_device(): row_grads = lax.psum(branch_part, 'ha').astype(jnp.bfloat16)  20.5 us
    dot_general x2, matrix products, tile_terms(): jnp.einsum('qd,kd->qk', query_rows, key_block, preferred_element_type=jnp...  9.21 us
    while x36, local copies, waits for them, and re-layouts  8.86 us
    convert_element_type x1, local copies, waits for them, and re-layouts, on_device(): query_grad = (softmax_scale * query_acc).astype(jnp.bfloat16).reshape(tok...  7.65 us
  transfers between devices with their start and end apart: 2, of which 2 were waited for; matrix products, arithmetic and copies ran while one was open for 10% of the time, Pallas kernels for 0%

commit v1 on v0

v1 whole, which is shorter than its diff:
```python
import jax
import jax.numpy as jnp
from jax import lax
from jax.experimental import pallas as pl
from jax.experimental.pallas import tpu as pltpu
from jax.sharding import PartitionSpec as P

BRANCH = 32
LANES = 128
GROUP = LANES // BRANCH
KEY_TILE = 256


softmax_scale = 192.0 ** (-0.5)

F32 = jnp.float32
BF16 = jnp.bfloat16


HBM = pl.BlockSpec(memory_space=pltpu.HBM)
VMEM = pl.BlockSpec(memory_space=pltpu.VMEM)
SMEM = pl.BlockSpec(memory_space=pltpu.SMEM)


def params(mib):
    return pltpu.CompilerParams(vmem_limit_bytes=mib * 1024 * 1024)


def cost(flops, nbytes):
    return pl.CostEstimate(flops=int(flops), bytes_accessed=int(nbytes), transcendentals=0)


def swap_matrix(shape=(GROUP * LANES, GROUP * LANES)):
    row = lax.broadcasted_iota(jnp.int32, shape, 0)
    col = lax.broadcasted_iota(jnp.int32, shape, 1)
    swapped = (
        jnp.bitwise_and(jnp.right_shift(col, 5), 3) * LANES
        + jnp.right_shift(col, 7) * BRANCH
        + jnp.bitwise_and(col, BRANCH - 1)
    )
    return jnp.where(row == swapped, F32(1), F32(0)).astype(BF16)


def pack_queries(queries_t):
    heads, width, tokens = queries_t.shape
    halves, groups, chunks = tokens // LANES, heads // GROUP, 6
    rows = width // chunks

    def body(q_hbm, out_ref, q_ref, sems, perm):
        def copy(d):
            at = pl.ds(pl.multiple_of(d * rows, 16), rows)
            return pltpu.make_async_copy(q_hbm.at[:, at, :], q_ref.at[:, at, :], sems.at[d])

        for d in range(chunks):
            copy(d).start()
        perm[...] = swap_matrix()

        @pl.loop(0, chunks)
        def _(d):
            copy(d).wait()
            at = pl.ds(pl.multiple_of(d * rows, 16), rows)
            wide = jnp.concatenate(
                [
                    jnp.concatenate(
                        [q_ref[g * GROUP + h, at, a * LANES : (a + 1) * LANES] for h in range(GROUP)],
                        axis=1,
                    )
                    for a in range(halves)
                    for g in range(groups)
                ],
                axis=0,
            )
            mixed = jnp.dot(wide, perm[...], preferred_element_type=F32).astype(BF16)
            for a in range(halves):
                for g in range(groups):
                    top = (a * groups + g) * rows
                    for b in range(GROUP):
                        out_ref[a * GROUP + b, at, g * LANES : (g + 1) * LANES] = mixed[
                            top : top + rows, b * LANES : (b + 1) * LANES
                        ]

    return pl.pallas_call(
        body,
        in_specs=[HBM],
        out_specs=VMEM,
        out_shape=jax.ShapeDtypeStruct((tokens // BRANCH, width, heads * BRANCH), BF16),
        scratch_shapes=[
            pltpu.VMEM((heads, width, tokens), BF16),
            pltpu.SemaphoreType.DMA((chunks,)),
            pltpu.VMEM((GROUP * LANES, GROUP * LANES), BF16),
        ],
        compiler_params=params(16),
        cost_estimate=cost(2 * heads * tokens * width * 512, 4 * heads * tokens * width),
        name="pack_queries",
    )(pltpu.with_memory_space_constraint(queries_t, pltpu.HBM))


def pack_grads(grad_rows, saved_rows, heads):
    rows, rank = grad_rows.shape
    cols = heads * BRANCH
    branches = rows // cols
    head_bits = heads.bit_length() - 1

    def body(g_hbm, o_hbm, out_ref, delta_ref, g_ref, o_ref, sems, perm):
        def copies(b):
            at = pl.ds(pl.multiple_of(b * cols, 16), cols)
            return (
                pltpu.make_async_copy(g_hbm.at[at, :], g_ref.at[at, :], sems.at[0, b]),
                pltpu.make_async_copy(o_hbm.at[at, :], o_ref.at[at, :], sems.at[1, b]),
            )

        for b in range(branches):
            for copy in copies(b):
                copy.start()
        row = lax.broadcasted_iota(jnp.int32, (cols, cols), 0)
        col = lax.broadcasted_iota(jnp.int32, (cols, cols), 1)
        source = jnp.left_shift(jnp.bitwise_and(col, BRANCH - 1), head_bits) + jnp.right_shift(col, 5)
        perm[...] = jnp.where(row == source, F32(1), F32(0)).astype(BF16)

        @pl.loop(0, branches)
        def _(b):
            for copy in copies(b):
                copy.wait()
            at = pl.ds(pl.multiple_of(b * cols, 16), cols)
            grads = g_ref[at, :]
            out_ref[b] = lax.dot_general(
                grads, perm[...], (((0,), (0,)), ((), ())), preferred_element_type=F32
            ).astype(BF16)
            delta = jnp.sum(o_ref[at, :].astype(F32) * grads.astype(F32), axis=1, keepdims=True)
            high = delta.astype(BF16)
            rest = delta - high.astype(F32)
            mid = rest.astype(BF16)
            low = (rest - mid.astype(F32)).astype(BF16)
            lane = lax.broadcasted_iota(jnp.int32, (cols, LANES), 1)
            parts = jnp.where(
                lane == 0,
                high.astype(F32),
                jnp.where(lane == 1, mid.astype(F32), jnp.where(lane == 2, low.astype(F32), F32(0))),
            ).astype(BF16)
            moved = lax.dot_general(
                parts, perm[...], (((0,), (0,)), ((), ())), preferred_element_type=F32
            )
            delta_ref[b] = moved[0:1] + moved[1:2] + moved[2:3]

    return pl.pallas_call(
        body,
        in_specs=[HBM, HBM],
        out_specs=[VMEM, VMEM],
        out_shape=[
            jax.ShapeDtypeStruct((branches, rank, cols), BF16),
            jax.ShapeDtypeStruct((branches, 1, cols), F32),
        ],
        scratch_shapes=[
            pltpu.VMEM((rows, rank), BF16),
            pltpu.VMEM((rows, rank), BF16),
            pltpu.SemaphoreType.DMA((2, branches)),
            pltpu.VMEM((cols, cols), BF16),
        ],
        compiler_params=params(20),
        cost_estimate=cost(2 * rows * rank * cols, 6 * rows * rank),
        name="pack_grads",
    )(
        pltpu.with_memory_space_constraint(grad_rows, pltpu.HBM),
        pltpu.with_memory_space_constraint(saved_rows, pltpu.HBM),
    )


def attend(place, parents, own_keys, other_keys, packed_q, packed_g, lse, deltas, sizes):
    ba, ha = sizes
    columns = ba // 2
    branches, width, cols = packed_q.shape
    rank = packed_g.shape[1]
    slots, piece, _ = own_keys.shape
    prefix = 2 * slots * piece
    key_tile = min(KEY_TILE, prefix)
    tiles = prefix // key_tile
    keys_ba = prefix // ba
    width_ba = width // ba
    half = width * keys_ba // LANES
    payload = 2 * half
    part = payload // ha

    def body(place_ref, parents_ref, own_ref, other_ref, q_ref, g_ref, lse_ref, delta_ref,
             send_ref, score_ref, keys, acc_q, acc_g, pack):
        me_ba, me_ha = place_ref[0], place_ref[1]
        me_col, me_core = jnp.right_shift(me_ba, 1), jnp.bitwise_and(me_ba, 1)

        for core_at, ref in enumerate((own_ref, other_ref)):
            for hr in range(ha):
                for zr in range(columns):
                    ba_at = 2 * jnp.bitwise_xor(me_col, zr) + jnp.bitwise_xor(me_core, core_at)
                    at = ba_at * ha + jnp.bitwise_xor(me_ha, hr)
                    keys[pl.ds(pl.multiple_of(at * piece, piece), piece), :] = ref[hr * columns + zr]
        acc_q[...] = jnp.zeros_like(acc_q)
        acc_g[...] = jnp.zeros_like(acc_g)

        @pl.loop(0, branches)
        def _(b):
            limit = parents_ref[b * BRANCH]
            for kt in range(tiles):
                rows = slice(kt * key_tile, (kt + 1) * key_tile)

                @pl.when(limit >= kt * key_tile)
                def _(rows=rows, kt=kt):
                    key_block = keys[rows, :]
                    scores = jnp.dot(key_block, q_ref[b], preferred_element_type=F32) * softmax_scale
                    at = kt * key_tile + lax.broadcasted_iota(jnp.int32, scores.shape, 0)
                    prob = jnp.where(at <= limit, jnp.exp(scores - lse_ref[b]), F32(0))
                    grad_prob = jnp.dot(key_block[:, :rank], g_ref[b], preferred_element_type=F32)
                    grad_score = (prob * (grad_prob - delta_ref[b])).astype(BF16)
                    score_ref[b, rows, :] = grad_score
                    across = (((1,), (1,)), ((), ()))
                    acc_q[:, rows] += lax.dot_general(
                        q_ref[b], grad_score, across, preferred_element_type=F32
                    )
                    acc_g[:, rows] += lax.dot_general(
                        g_ref[b], prob.astype(BF16), across, preferred_element_type=F32
                    )

                @pl.when(limit < kt * key_tile)
                def _(rows=rows):
                    score_ref[b, rows, :] = jnp.zeros((key_tile, cols), BF16)

        acc_q[...] = acc_q[...] * softmax_scale
        acc_q[:rank, :] += acc_g[...]
        lane = lax.broadcasted_iota(jnp.int32, (half, LANES), 1)
        per_tile = LANES // keys_ba
        for at in range(ba):
            tile = acc_q[:, (at // per_tile) * LANES : (at // per_tile + 1) * LANES]
            first = at % per_tile
            block = jnp.zeros((half, LANES), F32)
            for s in range(per_tile):
                strip = tile[s * half : (s + 1) * half, :]
                shift = ((s - first) * keys_ba) % LANES
                if shift:
                    strip = pltpu.roll(strip, shift, axis=1)
                block = jnp.where((lane >= s * keys_ba) & (lane < (s + 1) * keys_ba), strip, block)
            pack[:half, :] = block
            for l in range(prefix // LANES):
                pack[half + l * width_ba : half + (l + 1) * width_ba, :] = acc_q[
                    at * width_ba : (at + 1) * width_ba, l * LANES : (l + 1) * LANES
                ]
            to_core = jnp.bitwise_xor(me_core, at % 2)
            to_col = jnp.bitwise_xor(me_col, at // 2)
            for h in range(ha):
                send_ref[to_core, jnp.bitwise_xor(me_ha, h), to_col] = pack[
                    h * part : (h + 1) * part, :
                ]

    return pl.pallas_call(
        body,
        in_specs=[SMEM, SMEM] + [VMEM] * 6,
        out_specs=[VMEM, VMEM, VMEM],
        out_shape=[
            jax.ShapeDtypeStruct((2, ha, columns, part, LANES), F32),
            jax.ShapeDtypeStruct((branches, prefix, cols), BF16),
            jax.ShapeDtypeStruct((prefix, width), BF16),
        ],
        scratch_shapes=[
            pltpu.VMEM((width, prefix), F32),
            pltpu.VMEM((rank, prefix), F32),
            pltpu.VMEM((payload, LANES), F32),
        ],
        compiler_params=params(24),
        cost_estimate=cost(8 * branches * cols * prefix * width, 3 * branches * cols * width * 2),
        name="attend",
    )(place, parents, own_keys, other_keys, packed_q, packed_g, lse, deltas)


def exchange(tiles):
    lane = lax.broadcasted_iota(jnp.int32, tiles[0].shape, 1)
    bit, tiles = GROUP // 2, list(tiles)
    while bit:
        width = bit * BRANCH
        low = jnp.bitwise_and(lane, width) == 0
        out = list(tiles)
        for at in range(GROUP):
            if not at & bit:
                a, b = tiles[at], tiles[at | bit]
                out[at] = jnp.where(low, a, pltpu.roll(b, width, axis=1))
                out[at | bit] = jnp.where(low, pltpu.roll(a, LANES - width, axis=1), b)
        tiles, bit = out, bit // 2
    return tiles


def query_gradient(before, steps, keys, grad_score, heads):
    branches, prefix, _ = grad_score.shape
    width = keys.shape[1]
    tokens = branches * BRANCH
    halves = tokens // LANES
    first, last = steps

    def body(k_ref, s_ref, *refs):
        out_hbm, keys_t, slots, sems = refs[-4:]
        keys_t[...] = jnp.transpose(k_ref[...], (1, 0))

        def copy(g):
            at = (g - first) % 2
            return pltpu.make_async_copy(
                slots.at[at], out_hbm.at[pl.ds(g * GROUP, GROUP)], sems.at[at]
            )

        for g in range(first, last):
            if g - first >= 2:
                copy(g - 2).wait()
            for a in range(halves):
                wide = jnp.concatenate(
                    [s_ref[a * GROUP + b, :, g * LANES : (g + 1) * LANES] for b in range(GROUP)], axis=1
                )
                grads = softmax_scale * jnp.dot(keys_t[...], wide, preferred_element_type=F32)
                tiles = exchange([grads[:, b * LANES : (b + 1) * LANES] for b in range(GROUP)])
                for h in range(GROUP):
                    slots[(g - first) % 2, h, :, a * LANES : (a + 1) * LANES] = tiles[h].astype(BF16)
            copy(g).start()
        for g in range(max(first, last - 2), last):
            copy(g).wait()

    return pl.pallas_call(
        body,
        in_specs=[VMEM, VMEM] + ([] if before is None else [HBM]),
        out_specs=HBM,
        out_shape=jax.ShapeDtypeStruct((heads, width, tokens), BF16),
        input_output_aliases={} if before is None else {2: 0},
        scratch_shapes=[
            pltpu.VMEM((width, prefix), BF16),
            pltpu.VMEM((2, GROUP, width, tokens), BF16),
            pltpu.SemaphoreType.DMA((2,)),
        ],
        compiler_params=params(16),
        cost_estimate=cost(
            2 * (last - first) * GROUP * tokens * prefix * width, (last - first) * GROUP * tokens * width * 2
        ),
        name="query_gradient",
    )(keys, grad_score, *([] if before is None else [before]))


def project(place, parts, hidden_sets, order, latent_weight, sizes, prefix):
    ba, ha = sizes
    width, columns = latent_weight.shape
    keys_ba, width_ba = prefix // ba, width // ba
    part = parts[0].shape[0]
    half = part * ha // 2

    def body(place_ref, *refs):
        part_refs = refs[:ha]
        own_ref, other_ref, weight_ref, wgrad_ref, igrad_ref, pack, hid = refs[ha:]
        me_ba, me_ha = place_ref[0], place_ref[1]
        for hr in range(ha):
            at = jnp.bitwise_xor(me_ha, hr) * part
            pack[pl.ds(pl.multiple_of(at, 8), part), :] = part_refs[hr][...].astype(F32)
        for core_at, ref in enumerate((own_ref, other_ref)):
            for slot, zr in enumerate(order):
                at = jnp.bitwise_xor(me_ba, 2 * zr + core_at) * keys_ba
                hid[pl.ds(pl.multiple_of(at, 8), keys_ba), :] = ref[slot]
        grad_columns = jnp.concatenate(
            [
                pack[half + l * width_ba : half + (l + 1) * width_ba, :]
                for l in range(prefix // LANES)
            ],
            axis=1,
        ).astype(BF16)
        wgrad_ref[...] = jnp.dot(grad_columns, hid[...], preferred_element_type=F32).astype(BF16)
        rows_t = jnp.concatenate(
            [
                pack[:half, s * keys_ba : (s + 1) * keys_ba]
                for s in range(LANES // keys_ba)
            ],
            axis=0,
        ).astype(BF16)
        igrad_ref[...] = lax.dot_general(
            rows_t, weight_ref[...], (((0,), (0,)), ((), ())), preferred_element_type=F32
        ).astype(BF16)

    return pl.pallas_call(
        body,
        in_specs=[SMEM] + [VMEM] * (ha + 3),
        out_specs=[VMEM, VMEM],
        out_shape=[
            jax.ShapeDtypeStruct((width_ba, columns), BF16),
            jax.ShapeDtypeStruct((keys_ba, columns), BF16),
        ],
        scratch_shapes=[
            pltpu.VMEM((part * ha, LANES), F32),
            pltpu.VMEM((prefix, columns), BF16),
        ],
        compiler_params=params(24),
        cost_estimate=cost(4 * width * keys_ba * columns, 4 * width * columns),
        name="project",
    )(place, *parts, *hidden_sets, latent_weight)


def on_device(sizes, queries, out_grad, out_saved, logsumexp, parents, latents, hidden, latent_weight):
    ba, ha = sizes
    columns = ba // 2
    tokens, heads, _ = queries.shape
    rank = out_grad.shape[2]
    branches, cols = tokens // BRANCH, heads * BRANCH
    prefix = latents.shape[0] * ba * ha

    def over_core(x):
        return lax.ppermute(x, "ba", [(i, i ^ 1) for i in range(ba)])

    def over_column(x, k):
        return lax.ppermute(x, "ba", [(i, i ^ (2 * k)) for i in range(ba)])

    def over_ha(x, k):
        return lax.ppermute(x, "ha", [(i, i ^ k) for i in range(ha)])

    def total(terms):
        return sum(t.astype(F32) for t in terms).astype(BF16)

    place = jnp.stack([lax.axis_index("ba"), lax.axis_index("ha")]).astype(jnp.int32)

    keys = jnp.stack([latents] + [over_column(latents, k) for k in range(1, columns)])
    keys = jnp.concatenate([keys] + [over_ha(keys, k) for k in range(1, ha)])
    other_keys = over_core(keys)

    packed_q = pack_queries(jnp.transpose(queries, (1, 2, 0)))
    packed_g, deltas = pack_grads(
        out_grad.reshape(tokens * heads, rank), out_saved.reshape(tokens * heads, rank), heads
    )
    lse = jnp.transpose(logsumexp.T.reshape(heads, branches, BRANCH), (1, 0, 2)).reshape(branches, 1, cols)

    hidden_all, order = hidden[None], [0]
    step = columns // 2
    while step:
        hidden_all = jnp.concatenate([hidden_all, over_column(hidden_all, step)])
        order = order + [k ^ step for k in order]
        step //= 2
    other_hidden = over_core(hidden_all)

    send, grad_score, keys = attend(
        place, parents, keys, other_keys, packed_q, packed_g, lse, deltas, sizes
    )
    query_grad, groups = None, heads // GROUP
    for steps in ((0, 1), (1, groups)):
        query_grad = query_gradient(query_grad, steps, keys, grad_score, heads)

    chip = (send[0] + over_core(send[1])).astype(BF16)
    plane = total([chip[0]] + [over_ha(chip[k], k) for k in range(1, ha)])
    owned = total([plane[0]] + [over_column(plane[k], k) for k in range(1, columns)])
    parts = [owned] + [over_ha(owned, k) for k in range(1, ha)]
    weight_grad, input_grad = project(
        place, parts, (hidden_all, other_hidden), order, latent_weight, sizes, prefix
    )
    return (jnp.transpose(query_grad, (2, 0, 1)), weight_grad, input_grad)


def solution(mesh):
    sizes = (mesh.shape["ba"], mesh.shape["ha"])

    def step(*args):
        return on_device(sizes, *args)

    step = jax.shard_map(
        step,
        mesh=mesh,
        in_specs=(
            P("ba", "ha", None),
            P("ba", "ha", None),
            P("ba", "ha", None),
            P("ba", "ha"),
            P("ba"),
            P(("ba", "ha"), None),
            P("ba", "ha"),
            P(None, "ha"),
        ),
        out_specs=(P("ba", "ha", None), P("ba", "ha"), P("ba", "ha")),
        check_vma=False,
    )
    return step
```

time: 246 us -> 88.3 us (0.36)
  blocking collectives: 93.7 us -> 0 us
  local copies, waits for them, and re-layouts: 40.3 us -> 3.2 us
  Pallas kernels: 0 us -> 29.2 us
  matrix products: 28.7 us -> 0 us
  starting transfers between devices: 0.26 us -> 27 us
  waiting for transfers between devices: 52.8 us -> 27.4 us
  other arithmetic: 14.7 us -> 0.52 us
  between operations: 14.1 us -> 0.93 us
    all_gather x1 -> x0, blocking collectives: 73.2 us -> none  [on_device(): all_keys = lax.all_gather(latents, ('ba', 'ha'), axis=0, tiled=True)]
    pallas_call x0 -> x6, Pallas kernels: none -> 29.2 us  [the longest x1 9.68 us: attend(): pl.pallas_call(body, in_specs=[SMEM, SMEM] + [VMEM] * 6, out_specs=[VMEM,...]
    unnamed x3 -> x0, waiting for transfers between devices: 29.1 us -> none
    dot_general x12 -> x0, matrix products: 28.7 us -> none  [the longest x2 9.21 us: tile_terms(): jnp.einsum('qd,kd->qk', query_rows, key_block, preferred_element_type=jnp...]
    ppermute x0 -> x20, waiting for transfers between devices: none -> 27.4 us  [the longest x8 22.4 us: over_column(): return lax.ppermute(x, 'ba', [(i, i ^ 2 * k) for i in range(ba)])]
    ppermute x0 -> x20, starting transfers between devices: none -> 27 us  [the longest x8 13.8 us: over_column(): return lax.ppermute(x, 'ba', [(i, i ^ 2 * k) for i in range(ba)])]
    reduce_scatter x1 -> x0, waiting for transfers between devices: 23.7 us -> none  [on_device(): lax.psum_scatter(jnp.einsum('pl,ph->lh', row_grads, hidden, preferred_ele...]
    psum x1 -> x0, blocking collectives: 20.5 us -> none  [on_device(): row_grads = lax.psum(branch_part, 'ha').astype(jnp.bfloat16)]
  transfers between devices with their start and end apart: 2 -> 20, of which waited for: 2 -> 6; matrix products, arithmetic and copies ran while one was open for 10% -> 2% of each run, Pallas kernels for 0% -> 20%
where the time goes in v1:
time: 88.3 us; the launch traced here: 88.2 us
  Pallas kernels  29.2 us (33%)
  waiting for transfers between devices  27.4 us (31%)
  starting transfers between devices  27 us (31%)
  local copies, waits for them, and re-layouts  3.2 us (4%)
  between operations  0.93 us (1%)
    ppermute x8, waiting for transfers between devices, over_column(): return lax.ppermute(x, 'ba', [(i, i ^ 2 * k) for i in range(ba)])  22.4 us
    ppermute x8, starting transfers between devices, over_column(): return lax.ppermute(x, 'ba', [(i, i ^ 2 * k) for i in range(ba)])  13.8 us
    ppermute x9, starting transfers between devices, over_ha(): return lax.ppermute(x, 'ha', [(i, i ^ k) for i in range(ha)])  10.7 us
    pallas_call x1, Pallas kernels, attend(): pl.pallas_call(body, in_specs=[SMEM, SMEM] + [VMEM] * 6, out_specs=[VMEM,...  9.68 us
    pallas_call x2, Pallas kernels, query_gradient(): pl.pallas_call(body, in_specs=[VMEM, VMEM] + ([] if before is None else [...  6.65 us
    pallas_call x1, Pallas kernels, pack_grads(): pl.pallas_call(body, in_specs=[HBM, HBM], out_specs=[VMEM, VMEM], out_sha...  5.95 us
    ppermute x9, waiting for transfers between devices, over_ha(): return lax.ppermute(x, 'ha', [(i, i ^ k) for i in range(ha)])  5 us
    pallas_call x1, Pallas kernels, pack_queries(): pl.pallas_call(body, in_specs=[HBM], out_specs=VMEM, out_shape=jax.ShapeD...  4.77 us
  transfers between devices with their start and end apart: 20, of which 6 were waited for; matrix products, arithmetic and copies ran while one was open for 2% of the time, Pallas kernels for 20%

profile of v1, /device:TPU:0, one launch (start us, length us, event | category | flops | bytes accessed | tf_op | source)
XLA Modules:
  0.0 88.2 jit_solution(14870660575120824555)
XLA Ops:
  0.6 3.1 %collective-permute-start = (bf16[16,576]{1,0:T(8,128)(2,1)}, bf16[16,576]{1,0:T(8,128)(2,1)S(1)}, u32[]{:S(2)}, u32[]{:S(2)}) collective-permute-start(bf16[16,576]{1,0:T(8,128)(2,1)} %param.13), channel_id=1, source_target_pairs={{0,8},{4,12},{8,0},{12,4},{16,24},{20,28},{24,16},{28,20},{1,9},{5... | collective-permute-start | bytes 55304 | tf_op jit(solution)/shard_map/ppermute | solution.py:404
  3.7 2.6 %collective-permute-start.1 = (bf16[16,576]{1,0:T(8,128)(2,1)}, bf16[16,576]{1,0:T(8,128)(2,1)S(1)}, u32[]{:S(2)}, u32[]{:S(2)}) collective-permute-start(bf16[16,576]{1,0:T(8,128)(2,1)} %param.13), channel_id=1, source_target_pairs={{0,16},{4,20},{8,24},{12,28},{16,0},{20,4},{24,8},{28,12},{1,17},{... | collective-permute-start | bytes 55304 | tf_op jit(solution)/shard_map/ppermute | solution.py:404
  6.3 0.0 collective-permute-start.2
  6.3 0.8 constant_dynamic-update-slice_fusion.6
  7.1 6.0 %pack_grads.1 = (bf16[8,512,512]{2,1,0:T(8,128)(2,1)S(1)}, f32[8,1,512]{2,1,0:T(1,128)S(1)}) custom-call(bf16[4096,512]{1,0:T(8,128)(2,1)} %bitcast.49, bf16[4096,512]{1,0:T(8,128)(2,1)} %bitcast.50), custom_call_target="tpu_custom_call" | custom-call | flops 2147483648 | bytes 12582912 | tf_op jit(solution)/shard_map/pack_grads/pallas_call | solution.py:145
  13.1 0.0 copy-start.1
  13.1 2.0 %copy-done.1 = bf16[8,512,512]{2,1,0:T(8,128)(2,1)} copy-done((bf16[8,512,512]{2,1,0:T(8,128)(2,1)}, bf16[8,512,512]{2,1,0:T(8,128)(2,1)S(1)}, u32[]{:S(2)}) %copy-start.1) | copy-done | bytes 4194328
  15.1 0.0 copy-done.6
  15.1 0.1 reshape.24
  15.2 0.1 reshape.25.lse_ref
  15.3 0.0 collective-permute-done
  15.3 0.0 collective-permute-done.1
  15.3 0.0 collective-permute-done.2
  15.3 0.0 copy-done.5
  15.4 1.7 %collective-permute-start.3 = (bf16[4,16,576]{2,1,0:T(8,128)(2,1)S(1)}, bf16[4,16,576]{2,1,0:T(8,128)(2,1)S(1)}, u32[]{:S(2)}, u32[]{:S(2)}) collective-permute-start(bf16[4,16,576]{2,1,0:T(8,128)(2,1)S(1)} %pad_maximum_fusion.2), channel_id=1, source_target_pairs={{0,1},{1,0},{2,3},{3,2},{4,5},{5,4},{6,7},{7,6},{8,9},{9,8},{10,11... | collective-permute-start | bytes 221192 | tf_op jit(solution)/shard_map/ppermute | solution.py:407
  17.1 1.5 %collective-permute-start.4 = (bf16[4,16,576]{2,1,0:T(8,128)(2,1)S(1)}, bf16[4,16,576]{2,1,0:T(8,128)(2,1)S(1)}, u32[]{:S(2)}, u32[]{:S(2)}) collective-permute-start(bf16[4,16,576]{2,1,0:T(8,128)(2,1)S(1)} %pad_maximum_fusion.2), channel_id=1, source_target_pairs={{0,2},{1,3},{2,0},{3,1},{4,6},{5,7},{6,4},{7,5},{8,10},{9,11},{10,... | collective-permute-start | bytes 221192 | tf_op jit(solution)/shard_map/ppermute | solution.py:407
  18.6 0.3 collective-permute-start.5
  19.0 1.1 %collective-permute-done.3 = bf16[4,16,576]{2,1,0:T(8,128)(2,1)S(1)} collective-permute-done((bf16[4,16,576]{2,1,0:T(8,128)(2,1)S(1)}, bf16[4,16,576]{2,1,0:T(8,128)(2,1)S(1)}, u32[]{:S(2)}, u32[]{:S(2)}) %collective-permute-start.3) | collective-permute-done | bytes 73760 | tf_op jit(solution)/shard_map/ppermute | solution.py:407
  20.1 2.3 %collective-permute-done.4 = bf16[4,16,576]{2,1,0:T(8,128)(2,1)S(1)} collective-permute-done((bf16[4,16,576]{2,1,0:T(8,128)(2,1)S(1)}, bf16[4,16,576]{2,1,0:T(8,128)(2,1)S(1)}, u32[]{:S(2)}, u32[]{:S(2)}) %collective-permute-start.4) | collective-permute-done | bytes 73760 | tf_op jit(solution)/shard_map/ppermute | solution.py:407
  22.4 1.5 %collective-permute-done.5 = bf16[4,16,576]{2,1,0:T(8,128)(2,1)S(1)} collective-permute-done((bf16[4,16,576]{2,1,0:T(8,128)(2,1)S(1)}, bf16[4,16,576]{2,1,0:T(8,128)(2,1)S(1)}, u32[]{:S(2)}, u32[]{:S(2)}) %collective-permute-start.5) | collective-permute-done | bytes 73760 | tf_op jit(solution)/shard_map/ppermute | solution.py:407
  24.0 0.1 collective-permute-start.6
  24.1 0.1 pad_add_fusion.place_ref
  24.2 4.8 %pack_queries.1.q_ref = bf16[8,576,512]{2,1,0:T(8,128)(2,1)S(1)} custom-call(bf16[16,576,256]{2,1,0:T(8,128)(2,1)} %bitcast.48), custom_call_target="tpu_custom_call" | custom-call | flops 2415919104 | bytes 9437184 | tf_op jit(solution)/shard_map/pack_queries/pallas_call | solution.py:82
  28.9 0.0 collective-permute-done.6.other_ref
  29.0 0.0 copy-done.2
  29.0 0.0 copy-done.3
  29.0 9.7 %attend.1 = (f32[2,4,4,144,128]{4,3,2,1,0:T(8,128)S(1)}, bf16[8,512,512]{2,1,0:T(8,128)(2,1)S(1)}, bf16[512,576]{1,0:T(8,128)(2,1)S(1)}) custom-call(s32[2]{0:T(128)S(1)} %pad_add_fusion.place_ref, s32[256]{0:T(256)S(1)} %copy-done.3, bf16[16,16,576]{2,1,0:T(8,128)(2,1)S(1)} %constant_dynamic-update-slice_fusion.own_ref, ...), custom_call_target="tpu_custom_call" | custom-call | flops 9663676416 | bytes 14155776 | tf_op jit(solution)/shard_map/attend/pallas_call | solution.py:250
  38.7 0.0 copy-start.4
  38.7 0.1 slice_bitcast_fusion
  38.8 2.3 %collective-permute-start.7 = (f32[4,4,144,128]{3,2,1,0:T(8,128)S(1)}, f32[4,4,144,128]{3,2,1,0:T(8,128)S(1)}, u32[]{:S(2)}, u32[]{:S(2)}) collective-permute-start(f32[4,4,144,128]{3,2,1,0:T(8,128)S(1)} %slice_bitcast_fusion), channel_id=1, source_target_pairs={{0,4},{4,0},{8,12},{12,8},{16,20},{20,16},{24,28},{28,24},{1,5},{5... | collective-permute-start | bytes 3538952 | tf_op jit(solution)/shard_map/ppermute | solution.py:401
  41.1 0.0 copy-done.4
  41.1 3.5 %collective-permute-start.17 = (bf16[1,64,1792]{2,1,0:T(8,128)(2,1)S(1)}, bf16[1,64,1792]{2,1,0:T(8,128)(2,1)S(1)}, u32[]{:S(2)}, u32[]{:S(2)}) collective-permute-start(bf16[1,64,1792]{2,1,0:T(8,128)(2,1)S(1)} %bitcast.51), channel_id=1, source_target_pairs={{0,16},{4,20},{8,24},{12,28},{16,0},{20,4},{24,8},{28,12},{1,17},{... | collective-permute-start | bytes 688136 | tf_op jit(solution)/shard_map/ppermute | solution.py:404
  44.5 11.3 %collective-permute-done.17 = bf16[1,64,1792]{2,1,0:T(8,128)(2,1)S(1)} collective-permute-done((bf16[1,64,1792]{2,1,0:T(8,128)(2,1)S(1)}, bf16[1,64,1792]{2,1,0:T(8,128)(2,1)S(1)}, u32[]{:S(2)}, u32[]{:S(2)}) %collective-permute-start.17) | collective-permute-done | bytes 229408 | tf_op jit(solution)/shard_map/ppermute | solution.py:404
  55.9 0.2 collective-permute-start.18
  56.1 0.0 collective-permute-done.7
  56.1 0.2 fusion
  56.3 0.6 collective-permute-start.10
  56.9 1.5 %collective-permute-start.8 = (bf16[4,144,128]{2,1,0:T(8,128)(2,1)S(1)}, bf16[4,144,128]{2,1,0:T(8,128)(2,1)S(1)}, u32[]{:S(2)}, u32[]{:S(2)}) collective-permute-start(bf16[4,144,128]{2,1,0:T(8,128)(2,1)S(1)} %get-tuple-element.17), channel_id=1, source_target_pairs={{0,1},{1,0},{2,3},{3,2},{4,5},{5,4},{6,7},{7,6},{8,9},{9,8},{10,11... | collective-permute-start | bytes 442376 | tf_op jit(solution)/shard_map/ppermute | solution.py:407
  58.4 1.5 %collective-permute-start.9 = (bf16[4,144,128]{2,1,0:T(8,128)(2,1)S(1)}, bf16[4,144,128]{2,1,0:T(8,128)(2,1)S(1)}, u32[]{:S(2)}, u32[]{:S(2)}) collective-permute-start(bf16[4,144,128]{2,1,0:T(8,128)(2,1)S(1)} %get-tuple-element.19), channel_id=1, source_target_pairs={{0,2},{1,3},{2,0},{3,1},{4,6},{5,7},{6,4},{7,5},{8,10},{9,11},{10,... | collective-permute-start | bytes 442376 | tf_op jit(solution)/shard_map/ppermute | solution.py:407
  59.9 8.6 %collective-permute-done.18 = bf16[2,64,1792]{2,1,0:T(8,128)(2,1)S(1)} collective-permute-done((bf16[2,64,1792]{2,1,0:T(8,128)(2,1)S(1)}, bf16[2,64,1792]{2,1,0:T(8,128)(2,1)S(1)}, u32[]{:S(2)}, u32[]{:S(2)}) %collective-permute-start.18) | collective-permute-done | bytes 458784 | tf_op jit(solution)/shard_map/ppermute | solution.py:404
  68.5 0.1 pad_maximum_fusion.refs_4_
  68.6 0.1 collective-permute-start.19
  68.7 0.0 collective-permute-done.10
  68.7 0.0 collective-permute-done.8
  68.7 0.0 collective-permute-done.9
  68.7 0.1 fusion.3
  68.8 0.4 collective-permute-start.11
  69.1 3.0 %collective-permute-start.12 = (bf16[144,128]{1,0:T(8,128)(2,1)S(1)}, bf16[144,128]{1,0:T(8,128)(2,1)S(1)}, u32[]{:S(2)}, u32[]{:S(2)}) collective-permute-start(bf16[144,128]{1,0:T(8,128)(2,1)S(1)} %get-tuple-element.22), channel_id=1, source_target_pairs={{0,16},{4,20},{8,24},{12,28},{16,0},{20,4},{24,8},{28,12},{1,17},{... | collective-permute-start | bytes 110600 | tf_op jit(solution)/shard_map/ppermute | solution.py:404
  72.2 1.1 %collective-permute-start.13 = (bf16[144,128]{1,0:T(8,128)(2,1)S(1)}, bf16[144,128]{1,0:T(8,128)(2,1)S(1)}, u32[]{:S(2)}, u32[]{:S(2)}) collective-permute-start(bf16[144,128]{1,0:T(8,128)(2,1)S(1)} %get-tuple-element.21), channel_id=1, source_target_pairs={{0,24},{4,28},{8,16},{12,20},{16,8},{20,12},{24,0},{28,4},{1,25},{... | collective-permute-start | bytes 110600 | tf_op jit(solution)/shard_map/ppermute | solution.py:404
  73.2 2.2 %query_gradient.2.refs_0_ = bf16[16,576,256]{2,1,0:T(8,128)(2,1)} custom-call(bf16[512,576]{1,0:T(8,128)(2,1)S(1)} %get-tuple-element.12.k_ref, bf16[8,512,512]{2,1,0:T(8,128)(2,1)S(1)} %get-tuple-element.13.s_ref), custom_call_target="tpu_custom_call" | custom-call | flops 603979776 | bytes 1179648 | tf_op jit(solution)/shard_map/query_gradient/pallas_call | solution.py:318
  75.5 0.0 collective-permute-done.11
  75.5 0.0 collective-permute-done.12
  75.5 2.5 %collective-permute-done.13 = bf16[144,128]{1,0:T(8,128)(2,1)S(1)} collective-permute-done((bf16[144,128]{1,0:T(8,128)(2,1)S(1)}, bf16[144,128]{1,0:T(8,128)(2,1)S(1)}, u32[]{:S(2)}, u32[]{:S(2)}) %collective-permute-start.13) | collective-permute-done | bytes 36896 | tf_op jit(solution)/shard_map/ppermute | solution.py:404
  78.0 0.0 copy-start
  78.0 0.6 collective-permute-start.14
  78.6 0.5 collective-permute-start.15
  79.1 2.4 %collective-permute-start.16 = (bf16[144,128]{1,0:T(8,128)(2,1)S(1)}, bf16[144,128]{1,0:T(8,128)(2,1)S(1)}, u32[]{:S(2)}, u32[]{:S(2)}) collective-permute-start(bf16[144,128]{1,0:T(8,128)(2,1)S(1)} %fusion.6.refs_0_), channel_id=1, source_target_pairs={{0,3},{1,2},{2,1},{3,0},{4,7},{5,6},{6,5},{7,4},{8,11},{9,10},{10,... | collective-permute-start | bytes 110600 | tf_op jit(solution)/shard_map/ppermute | solution.py:407
  81.5 4.4 %query_gradient.3 = bf16[16,576,256]{2,1,0:T(8,128)(2,1)} custom-call(bf16[512,576]{1,0:T(8,128)(2,1)S(1)} %get-tuple-element.12.k_ref, bf16[8,512,512]{2,1,0:T(8,128)(2,1)S(1)} %get-tuple-element.13.s_ref, bf16[16,576,256]{2,1,0:T(8,128)(2,1)} %query_gradient.2.refs_0_), custom_call_target="tpu_custom_call", output_to_operand_aliasing={{}: (2, {})} | custom-call | flops 1811939328 | bytes 3538944 | tf_op jit(solution)/shard_map/query_gradient/pallas_call | solution.py:318
  86.0 0.0 collective-permute-done.19.refs_5_
  86.0 0.0 collective-permute-done.14.refs_1_
  86.0 0.0 collective-permute-done.15.refs_2_
  86.0 0.0 collective-permute-done.16.refs_3_
  86.0 0.0 copy-done
  86.0 2.1 %project.1 = (bf16[72,1792]{1,0:T(8,128)(2,1)}, bf16[64,1792]{1,0:T(8,128)(2,1)}) custom-call(s32[2]{0:T(128)S(1)} %pad_add_fusion.place_ref, bf16[144,128]{1,0:T(8,128)(2,1)S(1)} %fusion.6.refs_0_, bf16[144,128]{1,0:T(8,128)(2,1)S(1)} %collective-permute-done.14.refs_1_, bf16[144,128]{1,0:T(8,128)(2,1)S(1)} %collective-permute-done.15.refs_2_, ...), custom_call_target="tpu_custom_call" | custom-call | flops 264241152 | bytes 4128768 | tf_op jit(solution)/shard_map/project/pallas_call | solution.py:374
  (16 shorter events, 0.2 us)
Async XLA Ops:
  0.6 14.7 %collective-permute-start = (bf16[16,576]{1,0:T(8,128)(2,1)}, bf16[16,576]{1,0:T(8,128)(2,1)S(1)}, u32[]{:S(2)}, u32[]{:S(2)}) collective-permute-start(bf16[16,576]{1,0:T(8,128)(2,1)} %param.13), channel_id=1, source_target_pairs={{0,8},{4,12},{8,0},{12,4},{16,24},{20,28},{24,16},{28,20},{1,9},{5... | collective-permute-start | bytes 55304 | tf_op jit(solution)/shard_map/ppermute | solution.py:404
  3.7 11.6 %collective-permute-start.1 = (bf16[16,576]{1,0:T(8,128)(2,1)}, bf16[16,576]{1,0:T(8,128)(2,1)S(1)}, u32[]{:S(2)}, u32[]{:S(2)}) collective-permute-start(bf16[16,576]{1,0:T(8,128)(2,1)} %param.13), channel_id=1, source_target_pairs={{0,16},{4,20},{8,24},{12,28},{16,0},{20,4},{24,8},{28,12},{1,17},{... | collective-permute-start | bytes 55304 | tf_op jit(solution)/shard_map/ppermute | solution.py:404
  6.3 9.0 %collective-permute-start.2 = (bf16[16,576]{1,0:T(8,128)(2,1)}, bf16[16,576]{1,0:T(8,128)(2,1)S(1)}, u32[]{:S(2)}, u32[]{:S(2)}) collective-permute-start(bf16[16,576]{1,0:T(8,128)(2,1)} %param.13), channel_id=1, source_target_pairs={{0,24},{4,28},{8,16},{12,20},{16,8},{20,12},{24,0},{28,4},{1,25},{... | collective-permute-start | bytes 55304 | tf_op jit(solution)/shard_map/ppermute | solution.py:404
  7.1 8.0 %copy-start.6 = (f32[256,16]{0,1:T(8,128)S(1)}, f32[256,16]{0,1:T(8,128)}, u32[]{:S(2)}) copy-start(f32[256,16]{0,1:T(8,128)} %param.11) | copy-start | bytes 49156
  7.1 8.2 %copy-start.5 = (bf16[16,576]{1,0:T(8,128)(2,1)S(1)}, bf16[16,576]{1,0:T(8,128)(2,1)}, u32[]{:S(2)}) copy-start(bf16[16,576]{1,0:T(8,128)(2,1)} %param.13) | copy-start | bytes 55300
  13.1 2.0 %copy-start.1 = (bf16[8,512,512]{2,1,0:T(8,128)(2,1)}, bf16[8,512,512]{2,1,0:T(8,128)(2,1)S(1)}, u32[]{:S(2)}) copy-start(bf16[8,512,512]{2,1,0:T(8,128)(2,1)S(1)} %get-tuple-element.10.g_ref) | copy-start | bytes 12582916
  15.4 4.7 %collective-permute-start.3 = (bf16[4,16,576]{2,1,0:T(8,128)(2,1)S(1)}, bf16[4,16,576]{2,1,0:T(8,128)(2,1)S(1)}, u32[]{:S(2)}, u32[]{:S(2)}) collective-permute-start(bf16[4,16,576]{2,1,0:T(8,128)(2,1)S(1)} %pad_maximum_fusion.2), channel_id=1, source_target_pairs={{0,1},{1,0},{2,3},{3,2},{4,5},{5,4},{6,7},{7,6},{8,9},{9,8},{10,11... | collective-permute-start | bytes 221192 | tf_op jit(solution)/shard_map/ppermute | solution.py:407
  17.1 5.3 %collective-permute-start.4 = (bf16[4,16,576]{2,1,0:T(8,128)(2,1)S(1)}, bf16[4,16,576]{2,1,0:T(8,128)(2,1)S(1)}, u32[]{:S(2)}, u32[]{:S(2)}) collective-permute-start(bf16[4,16,576]{2,1,0:T(8,128)(2,1)S(1)} %pad_maximum_fusion.2), channel_id=1, source_target_pairs={{0,2},{1,3},{2,0},{3,1},{4,6},{5,7},{6,4},{7,5},{8,10},{9,11},{10,... | collective-permute-start | bytes 221192 | tf_op jit(solution)/shard_map/ppermute | solution.py:407
  18.6 5.3 %collective-permute-start.5 = (bf16[4,16,576]{2,1,0:T(8,128)(2,1)S(1)}, bf16[4,16,576]{2,1,0:T(8,128)(2,1)S(1)}, u32[]{:S(2)}, u32[]{:S(2)}) collective-permute-start(bf16[4,16,576]{2,1,0:T(8,128)(2,1)S(1)} %pad_maximum_fusion.2), channel_id=1, source_target_pairs={{0,3},{1,2},{2,1},{3,0},{4,7},{5,6},{6,5},{7,4},{8,11},{9,10},{10,... | collective-permute-start | bytes 221192 | tf_op jit(solution)/shard_map/ppermute | solution.py:407
  24.0 4.9 %collective-permute-start.6 = (bf16[16,16,576]{2,1,0:T(8,128)(2,1)S(1)}, bf16[16,16,576]{2,1,0:T(8,128)(2,1)S(1)}, u32[]{:S(2)}, u32[]{:S(2)}) collective-permute-start(bf16[16,16,576]{2,1,0:T(8,128)(2,1)S(1)} %constant_dynamic-update-slice_fusion.own_ref), channel_id=1, source_target_pairs={{0,4},{4,0},{8,12},{12,8},{16,20},{20,16},{24,28},{28,24},{1,5},{5... | collective-permute-start | bytes 884744 | tf_op jit(solution)/shard_map/ppermute | solution.py:401
  24.2 4.8 %copy-start.2 = (bf16[8,512,512]{2,1,0:T(8,128)(2,1)S(1)}, bf16[8,512,512]{2,1,0:T(8,128)(2,1)}, u32[]{:S(2)}) copy-start(bf16[8,512,512]{2,1,0:T(8,128)(2,1)} %copy-done.1) | copy-start | bytes 12582916
  24.2 4.8 %copy-start.3 = (s32[256]{0:T(256)S(1)}, s32[256]{0:T(256)}, u32[]{:S(2)}) copy-start(s32[256]{0:T(256)} %parents_ref.1) | copy-start | bytes 3076
  38.7 2.4 %copy-start.4 = (bf16[64,1792]{1,0:T(8,128)(2,1)S(1)}, bf16[64,1792]{1,0:T(8,128)(2,1)}, u32[]{:S(2)}) copy-start(bf16[64,1792]{1,0:T(8,128)(2,1)} %param.14) | copy-start | bytes 688132
  38.8 17.3 %collective-permute-start.7 = (f32[4,4,144,128]{3,2,1,0:T(8,128)S(1)}, f32[4,4,144,128]{3,2,1,0:T(8,128)S(1)}, u32[]{:S(2)}, u32[]{:S(2)}) collective-permute-start(f32[4,4,144,128]{3,2,1,0:T(8,128)S(1)} %slice_bitcast_fusion), channel_id=1, source_target_pairs={{0,4},{4,0},{8,12},{12,8},{16,20},{20,16},{24,28},{28,24},{1,5},{5... | collective-permute-start | bytes 3538952 | tf_op jit(solution)/shard_map/ppermute | solution.py:401
  41.1 14.7 %collective-permute-start.17 = (bf16[1,64,1792]{2,1,0:T(8,128)(2,1)S(1)}, bf16[1,64,1792]{2,1,0:T(8,128)(2,1)S(1)}, u32[]{:S(2)}, u32[]{:S(2)}) collective-permute-start(bf16[1,64,1792]{2,1,0:T(8,128)(2,1)S(1)} %bitcast.51), channel_id=1, source_target_pairs={{0,16},{4,20},{8,24},{12,28},{16,0},{20,4},{24,8},{28,12},{1,17},{... | collective-permute-start | bytes 688136 | tf_op jit(solution)/shard_map/ppermute | solution.py:404
  55.9 12.6 %collective-permute-start.18 = (bf16[2,64,1792]{2,1,0:T(8,128)(2,1)S(1)}, bf16[2,64,1792]{2,1,0:T(8,128)(2,1)S(1)}, u32[]{:S(2)}, u32[]{:S(2)}) collective-permute-start(bf16[2,64,1792]{2,1,0:T(8,128)(2,1)S(1)} %pad_maximum_fusion.1), channel_id=1, source_target_pairs={{0,8},{4,12},{8,0},{12,4},{16,24},{20,28},{24,16},{28,20},{1,9},{5... | collective-permute-start | bytes 1376264 | tf_op jit(solution)/shard_map/ppermute | solution.py:404
  56.3 12.3 %collective-permute-start.10 = (bf16[4,144,128]{2,1,0:T(8,128)(2,1)S(1)}, bf16[4,144,128]{2,1,0:T(8,128)(2,1)S(1)}, u32[]{:S(2)}, u32[]{:S(2)}) collective-permute-start(bf16[4,144,128]{2,1,0:T(8,128)(2,1)S(1)} %get-tuple-element.18), channel_id=1, source_target_pairs={{0,3},{1,2},{2,1},{3,0},{4,7},{5,6},{6,5},{7,4},{8,11},{9,10},{10,... | collective-permute-start | bytes 442376 | tf_op jit(solution)/shard_map/ppermute | solution.py:407
  56.9 11.8 %collective-permute-start.8 = (bf16[4,144,128]{2,1,0:T(8,128)(2,1)S(1)}, bf16[4,144,128]{2,1,0:T(8,128)(2,1)S(1)}, u32[]{:S(2)}, u32[]{:S(2)}) collective-permute-start(bf16[4,144,128]{2,1,0:T(8,128)(2,1)S(1)} %get-tuple-element.17), channel_id=1, source_target_pairs={{0,1},{1,0},{2,3},{3,2},{4,5},{5,4},{6,7},{7,6},{8,9},{9,8},{10,11... | collective-permute-start | bytes 442376 | tf_op jit(solution)/shard_map/ppermute | solution.py:407
  58.4 10.3 %collective-permute-start.9 = (bf16[4,144,128]{2,1,0:T(8,128)(2,1)S(1)}, bf16[4,144,128]{2,1,0:T(8,128)(2,1)S(1)}, u32[]{:S(2)}, u32[]{:S(2)}) collective-permute-start(bf16[4,144,128]{2,1,0:T(8,128)(2,1)S(1)} %get-tuple-element.19), channel_id=1, source_target_pairs={{0,2},{1,3},{2,0},{3,1},{4,6},{5,7},{6,4},{7,5},{8,10},{9,11},{10,... | collective-permute-start | bytes 442376 | tf_op jit(solution)/shard_map/ppermute | solution.py:407
  68.6 17.4 %collective-permute-start.19 = (bf16[4,64,1792]{2,1,0:T(8,128)(2,1)S(1)}, bf16[4,64,1792]{2,1,0:T(8,128)(2,1)S(1)}, u32[]{:S(2)}, u32[]{:S(2)}) collective-permute-start(bf16[4,64,1792]{2,1,0:T(8,128)(2,1)S(1)} %pad_maximum_fusion.refs_4_), channel_id=1, source_target_pairs={{0,4},{4,0},{8,12},{12,8},{16,20},{20,16},{24,28},{28,24},{1,5},{5... | collective-permute-start | bytes 2752520 | tf_op jit(solution)/shard_map/ppermute | solution.py:401
  68.8 6.7 %collective-permute-start.11 = (bf16[144,128]{1,0:T(8,128)(2,1)S(1)}, bf16[144,128]{1,0:T(8,128)(2,1)S(1)}, u32[]{:S(2)}, u32[]{:S(2)}) collective-permute-start(bf16[144,128]{1,0:T(8,128)(2,1)S(1)} %get-tuple-element.20), channel_id=1, source_target_pairs={{0,8},{4,12},{8,0},{12,4},{16,24},{20,28},{24,16},{28,20},{1,9},{5... | collective-permute-start | bytes 110600 | tf_op jit(solution)/shard_map/ppermute | solution.py:404
  69.1 6.3 %collective-permute-start.12 = (bf16[144,128]{1,0:T(8,128)(2,1)S(1)}, bf16[144,128]{1,0:T(8,128)(2,1)S(1)}, u32[]{:S(2)}, u32[]{:S(2)}) collective-permute-start(bf16[144,128]{1,0:T(8,128)(2,1)S(1)} %get-tuple-element.22), channel_id=1, source_target_pairs={{0,16},{4,20},{8,24},{12,28},{16,0},{20,4},{24,8},{28,12},{1,17},{... | collective-permute-start | bytes 110600 | tf_op jit(solution)/shard_map/ppermute | solution.py:404
  72.2 5.8 %collective-permute-start.13 = (bf16[144,128]{1,0:T(8,128)(2,1)S(1)}, bf16[144,128]{1,0:T(8,128)(2,1)S(1)}, u32[]{:S(2)}, u32[]{:S(2)}) collective-permute-start(bf16[144,128]{1,0:T(8,128)(2,1)S(1)} %get-tuple-element.21), channel_id=1, source_target_pairs={{0,24},{4,28},{8,16},{12,20},{16,8},{20,12},{24,0},{28,4},{1,25},{... | collective-permute-start | bytes 110600 | tf_op jit(solution)/shard_map/ppermute | solution.py:404
  78.0 8.1 %copy-start = (bf16[576,1792]{1,0:T(8,128)(2,1)S(1)}, bf16[576,1792]{1,0:T(8,128)(2,1)}, u32[]{:S(2)}) copy-start(bf16[576,1792]{1,0:T(8,128)(2,1)} %refs_6_.1) | copy-start | bytes 6193156
  78.0 8.0 %collective-permute-start.14 = (bf16[144,128]{1,0:T(8,128)(2,1)S(1)}, bf16[144,128]{1,0:T(8,128)(2,1)S(1)}, u32[]{:S(2)}, u32[]{:S(2)}) collective-permute-start(bf16[144,128]{1,0:T(8,128)(2,1)S(1)} %fusion.6.refs_0_), channel_id=1, source_target_pairs={{0,1},{1,0},{2,3},{3,2},{4,5},{5,4},{6,7},{7,6},{8,9},{9,8},{10,11... | collective-permute-start | bytes 110600 | tf_op jit(solution)/shard_map/ppermute | solution.py:407
  78.6 7.4 %collective-permute-start.15 = (bf16[144,128]{1,0:T(8,128)(2,1)S(1)}, bf16[144,128]{1,0:T(8,128)(2,1)S(1)}, u32[]{:S(2)}, u32[]{:S(2)}) collective-permute-start(bf16[144,128]{1,0:T(8,128)(2,1)S(1)} %fusion.6.refs_0_), channel_id=1, source_target_pairs={{0,2},{1,3},{2,0},{3,1},{4,6},{5,7},{6,4},{7,5},{8,10},{9,11},{10,... | collective-permute-start | bytes 110600 | tf_op jit(solution)/shard_map/ppermute | solution.py:407
  79.1 6.9 %collective-permute-start.16 = (bf16[144,128]{1,0:T(8,128)(2,1)S(1)}, bf16[144,128]{1,0:T(8,128)(2,1)S(1)}, u32[]{:S(2)}, u32[]{:S(2)}) collective-permute-start(bf16[144,128]{1,0:T(8,128)(2,1)S(1)} %fusion.6.refs_0_), channel_id=1, source_target_pairs={{0,3},{1,2},{2,1},{3,0},{4,7},{5,6},{6,5},{7,4},{8,11},{9,10},{10,... | collective-permute-start | bytes 110600 | tf_op jit(solution)/shard_map/ppermute | solution.py:407

commit v2 on v1

--- a/solution.py
+++ b/solution.py
@@ -39,6 +39,22 @@
         + jnp.bitwise_and(col, BRANCH - 1)
     )
     return jnp.where(row == swapped, F32(1), F32(0)).astype(BF16)
+
+
+def exchange(tiles):
+    lane = lax.broadcasted_iota(jnp.int32, tiles[0].shape, 1)
+    bit, tiles = GROUP // 2, list(tiles)
+    while bit:
+        width = bit * BRANCH
+        low = jnp.bitwise_and(lane, width) == 0
+        out = list(tiles)
+        for at in range(GROUP):
+            if not at & bit:
+                a, b = tiles[at], tiles[at | bit]
+                out[at] = jnp.where(low, a, pltpu.roll(b, width, axis=1))
+                out[at | bit] = jnp.where(low, pltpu.roll(a, LANES - width, axis=1), b)
+        tiles, bit = out, bit // 2
+    return tiles
 
 
 def pack_queries(queries_t):
@@ -95,13 +111,18 @@
     )(pltpu.with_memory_space_constraint(queries_t, pltpu.HBM))
 
 
-def pack_grads(grad_rows, saved_rows, heads):
+def pack_grads(grad_rows, saved_rows, lse_t):
+    heads, tokens = lse_t.shape
+    groups = heads // GROUP
     rows, rank = grad_rows.shape
     cols = heads * BRANCH
     branches = rows // cols
     head_bits = heads.bit_length() - 1
 
-    def body(g_hbm, o_hbm, out_ref, delta_ref, g_ref, o_ref, sems, perm):
+    def body(g_hbm, o_hbm, l_hbm, out_ref, delta_ref, lse_ref, g_ref, o_ref, l_ref, sems, l_sem, perm):
+        lse_copy = pltpu.make_async_copy(l_hbm, l_ref, l_sem)
+        lse_copy.start()
+
         def copies(b):
             at = pl.ds(pl.multiple_of(b * cols, 16), cols)
             return (
@@ -142,18 +163,35 @@
             )
             delta_ref[b] = moved[0:1] + moved[1:2] + moved[2:3]
 
+        lse_copy.wait()
+        for a in range(tokens // LANES):
+            tile = l_ref[:, a * LANES : (a + 1) * LANES]
+            picked = exchange(
+                [
+                    jnp.concatenate(
+                        [tile[g * GROUP + h : g * GROUP + h + 1] for g in range(groups)], axis=0
+                    )
+                    for h in range(GROUP)
+                ]
+            )
+            for b in range(GROUP):
+                lse_ref[a * GROUP + b] = picked[b]
+
     return pl.pallas_call(
         body,
-        in_specs=[HBM, HBM],
-        out_specs=[VMEM, VMEM],
+        in_specs=[HBM, HBM, HBM],
+        out_specs=[VMEM, VMEM, VMEM],
         out_shape=[
             jax.ShapeDtypeStruct((branches, rank, cols), BF16),
             jax.ShapeDtypeStruct((branches, 1, cols), F32),
+            jax.ShapeDtypeStruct((branches, groups, LANES), F32),
         ],
         scratch_shapes=[
             pltpu.VMEM((rows, rank), BF16),
             pltpu.VMEM((rows, rank), BF16),
+            pltpu.VMEM((heads, tokens), F32),
             pltpu.SemaphoreType.DMA((2, branches)),
+            pltpu.SemaphoreType.DMA,
             pltpu.VMEM((cols, cols), BF16),
         ],
         compiler_params=params(20),
@@ -162,6 +200,7 @@
     )(
         pltpu.with_memory_space_constraint(grad_rows, pltpu.HBM),
         pltpu.with_memory_space_constraint(saved_rows, pltpu.HBM),
+        pltpu.with_memory_space_constraint(lse_t, pltpu.HBM),
     )
 
 
@@ -197,29 +236,39 @@
         @pl.loop(0, branches)
         def _(b):
             limit = parents_ref[b * BRANCH]
+            lse_row = jnp.concatenate([lse_ref[b, g : g + 1] for g in range(cols // LANES)], axis=1)
             for kt in range(tiles):
-                rows = slice(kt * key_tile, (kt + 1) * key_tile)
-
-                @pl.when(limit >= kt * key_tile)
-                def _(rows=rows, kt=kt):
-                    key_block = keys[rows, :]
-                    scores = jnp.dot(key_block, q_ref[b], preferred_element_type=F32) * softmax_scale
-                    at = kt * key_tile + lax.broadcasted_iota(jnp.int32, scores.shape, 0)
-                    prob = jnp.where(at <= limit, jnp.exp(scores - lse_ref[b]), F32(0))
-                    grad_prob = jnp.dot(key_block[:, :rank], g_ref[b], preferred_element_type=F32)
-                    grad_score = (prob * (grad_prob - delta_ref[b])).astype(BF16)
-                    score_ref[b, rows, :] = grad_score
-                    across = (((1,), (1,)), ((), ()))
-                    acc_q[:, rows] += lax.dot_general(
-                        q_ref[b], grad_score, across, preferred_element_type=F32
-                    )
-                    acc_g[:, rows] += lax.dot_general(
-                        g_ref[b], prob.astype(BF16), across, preferred_element_type=F32
-                    )
-
-                @pl.when(limit < kt * key_tile)
-                def _(rows=rows):
-                    score_ref[b, rows, :] = jnp.zeros((key_tile, cols), BF16)
+                start = kt * key_tile
+                for size in (key_tile // 2, key_tile):
+                    low = start if size < key_tile else start + key_tile // 2
+                    wanted = limit >= low
+                    if size < key_tile:
+                        wanted &= limit < start + key_tile // 2
+
+                    @pl.when(wanted)
+                    def _(rows=slice(start, start + size), size=size, start=start):
+                        key_block = keys[rows, :]
+                        scores = jnp.dot(key_block, q_ref[b], preferred_element_type=F32) * softmax_scale
+                        at = start + lax.broadcasted_iota(jnp.int32, scores.shape, 0)
+                        prob = jnp.where(at <= limit, jnp.exp(scores - lse_row), F32(0))
+                        grad_prob = jnp.dot(key_block[:, :rank], g_ref[b], preferred_element_type=F32)
+                        grad_score = (prob * (grad_prob - delta_ref[b])).astype(BF16)
+                        score_ref[b, rows, :] = grad_score
+                        if size < key_tile:
+                            score_ref[b, start + size : start + key_tile, :] = jnp.zeros(
+                                (key_tile - size, cols), BF16
+                            )
+                        across = (((1,), (1,)), ((), ()))
+                        acc_q[:, rows] += lax.dot_general(
+                            q_ref[b], grad_score, across, preferred_element_type=F32
+                        )
+                        acc_g[:, rows] += lax.dot_general(
+                            g_ref[b], prob.astype(BF16), across, preferred_element_type=F32
+                        )
+
+                @pl.when(limit < start)
+                def _(start=start):
+                    score_ref[b, start : start + key_tile, :] = jnp.zeros((key_tile, cols), BF16)
 
         acc_q[...] = acc_q[...] * softmax_scale
         acc_q[:rank, :] += acc_g[...]
@@ -267,22 +316,6 @@
     )(place, parents, own_keys, other_keys, packed_q, packed_g, lse, deltas)
 
 
-def exchange(tiles):
-    lane = lax.broadcasted_iota(jnp.int32, tiles[0].shape, 1)
-    bit, tiles = GROUP // 2, list(tiles)
-    while bit:
-        width = bit * BRANCH
-        low = jnp.bitwise_and(lane, width) == 0
-        out = list(tiles)
-        for at in range(GROUP):
-            if not at & bit:
-                a, b = tiles[at], tiles[at | bit]
-                out[at] = jnp.where(low, a, pltpu.roll(b, width, axis=1))
-                out[at | bit] = jnp.where(low, pltpu.roll(a, LANES - width, axis=1), b)
-        tiles, bit = out, bit // 2
-    return tiles
-
-
 def query_gradient(before, steps, keys, grad_score, heads):
     branches, prefix, _ = grad_score.shape
     width = keys.shape[1]
@@ -340,10 +373,12 @@
     keys_ba, width_ba = prefix // ba, width // ba
     part = parts[0].shape[0]
     half = part * ha // 2
+    middle = -(-columns // 512) * 256
+    parts_of = (slice(0, middle), slice(middle, columns))
 
     def body(place_ref, *refs):
         part_refs = refs[:ha]
-        own_ref, other_ref, weight_ref, wgrad_ref, igrad_ref, pack, hid = refs[ha:]
+        own_ref, other_ref, weight_ref, wgrad_hbm, igrad_hbm, pack, hid, wrows, irows, sems = refs[ha:]
         me_ba, me_ha = place_ref[0], place_ref[1]
         for hr in range(ha):
             at = jnp.bitwise_xor(me_ha, hr) * part
@@ -359,7 +394,6 @@
             ],
             axis=1,
         ).astype(BF16)
-        wgrad_ref[...] = jnp.dot(grad_columns, hid[...], preferred_element_type=F32).astype(BF16)
         rows_t = jnp.concatenate(
             [
                 pack[:half, s * keys_ba : (s + 1) * keys_ba]
@@ -367,14 +401,28 @@
             ],
             axis=0,
         ).astype(BF16)
-        igrad_ref[...] = lax.dot_general(
-            rows_t, weight_ref[...], (((0,), (0,)), ((), ())), preferred_element_type=F32
-        ).astype(BF16)
+        copies = []
+
+        def send(buffer, out_hbm, at, value):
+            buffer[:, at] = value.astype(BF16)
+            copy = pltpu.make_async_copy(buffer.at[:, at], out_hbm.at[:, at], sems.at[len(copies)])
+            copy.start()
+            copies.append(copy)
+
+        for at in parts_of:
+            term = lax.dot_general(
+                rows_t, weight_ref[:, at], (((0,), (0,)), ((), ())), preferred_element_type=F32
+            )
+            send(irows, igrad_hbm, at, term)
+        for at in parts_of:
+            send(wrows, wgrad_hbm, at, jnp.dot(grad_columns, hid[:, at], preferred_element_type=F32))
+        for copy in copies:
+            copy.wait()
 
     return pl.pallas_call(
         body,
         in_specs=[SMEM] + [VMEM] * (ha + 3),
-        out_specs=[VMEM, VMEM],
+        out_specs=[HBM, HBM],
         out_shape=[
             jax.ShapeDtypeStruct((width_ba, columns), BF16),
             jax.ShapeDtypeStruct((keys_ba, columns), BF16),
@@ -382,6 +430,9 @@
         scratch_shapes=[
             pltpu.VMEM((part * ha, LANES), F32),
             pltpu.VMEM((prefix, columns), BF16),
+            pltpu.VMEM((width_ba, columns), BF16),
+            pltpu.VMEM((keys_ba, columns), BF16),
+            pltpu.SemaphoreType.DMA((4,)),
         ],
         compiler_params=params(24),
         cost_estimate=cost(4 * width * keys_ba * columns, 4 * width * columns),
@@ -394,7 +445,6 @@
     columns = ba // 2
     tokens, heads, _ = queries.shape
     rank = out_grad.shape[2]
-    branches, cols = tokens // BRANCH, heads * BRANCH
     prefix = latents.shape[0] * ba * ha
 
     def over_core(x):
@@ -412,19 +462,21 @@
     place = jnp.stack([lax.axis_index("ba"), lax.axis_index("ha")]).astype(jnp.int32)
 
     keys = jnp.stack([latents] + [over_column(latents, k) for k in range(1, columns)])
+    keys = lax.optimization_barrier(keys)
     keys = jnp.concatenate([keys] + [over_ha(keys, k) for k in range(1, ha)])
     other_keys = over_core(keys)
 
     packed_q = pack_queries(jnp.transpose(queries, (1, 2, 0)))
-    packed_g, deltas = pack_grads(
-        out_grad.reshape(tokens * heads, rank), out_saved.reshape(tokens * heads, rank), heads
+    packed_g, deltas, lse = pack_grads(
+        out_grad.reshape(tokens * heads, rank), out_saved.reshape(tokens * heads, rank), logsumexp.T
     )
-    lse = jnp.transpose(logsumexp.T.reshape(heads, branches, BRANCH), (1, 0, 2)).reshape(branches, 1, cols)
 
     hidden_all, order = hidden[None], [0]
     step = columns // 2
     while step:
         hidden_all = jnp.concatenate([hidden_all, over_column(hidden_all, step)])
+        if step > 1:
+            place, hidden_all = lax.optimization_barrier((place, hidden_all))
         order = order + [k ^ step for k in order]
         step //= 2
     other_hidden = over_core(hidden_all)

time: 88.3 us -> 76.5 us (0.87)
  waiting for transfers between devices: 27.4 us -> 10.1 us
  local copies, waits for them, and re-layouts: 3.2 us -> 8.86 us
    ppermute x8, waiting for transfers between devices: 22.4 us -> 8.14 us  [over_column(): return lax.ppermute(x, 'ba', [(i, i ^ 2 * k) for i in range(ba)])]
    unnamed x20 -> x17, local copies, waits for them, and re-layouts: 2.88 us -> 8.71 us
    ppermute x9, waiting for transfers between devices: 5 us -> 0.22 us  [over_ha(): return lax.ppermute(x, 'ha', [(i, i ^ k) for i in range(ha)])]
    ppermute x3, waiting for transfers between devices: 0.01 us -> 1.72 us  [over_core(): return lax.ppermute(x, 'ba', [(i, i ^ 1) for i in range(ba)])]
  transfers between devices with their start and end apart: 20 -> 20, of which waited for: 6 -> 6; matrix products, arithmetic and copies ran while one was open for 2% -> 1% of each run, Pallas kernels for 20% -> 23%
where the time goes in v2:
time: 76.5 us; the launch traced here: 76.3 us
  Pallas kernels  28.5 us (37%)
  starting transfers between devices  27.6 us (36%)
  waiting for transfers between devices  10.1 us (13%)
  local copies, waits for them, and re-layouts  8.86 us (12%)
  between operations  0.85 us (1%)
    ppermute x8, starting transfers between devices, over_column(): return lax.ppermute(x, 'ba', [(i, i ^ 2 * k) for i in range(ba)])  14.5 us
    ppermute x9, starting transfers between devices, over_ha(): return lax.ppermute(x, 'ha', [(i, i ^ k) for i in range(ha)])  10.7 us
    pallas_call x1, Pallas kernels, attend(): pl.pallas_call(body, in_specs=[SMEM, SMEM] + [VMEM] * 6, out_specs=[VMEM,...  8.9 us
    unnamed x17, local copies, waits for them, and re-layouts  8.71 us
    ppermute x8, waiting for transfers between devices, over_column(): return lax.ppermute(x, 'ba', [(i, i ^ 2 * k) for i in range(ba)])  8.14 us
    pallas_call x2, Pallas kernels, query_gradient(): pl.pallas_call(body, in_specs=[VMEM, VMEM] + ([] if before is None else [...  6.65 us
    pallas_call x1, Pallas kernels, pack_grads(): pl.pallas_call(body, in_specs=[HBM, HBM, HBM], out_specs=[VMEM, VMEM, VME...  6.12 us
    pallas_call x1, Pallas kernels, pack_queries(): pl.pallas_call(body, in_specs=[HBM], out_specs=VMEM, out_shape=jax.ShapeD...  4.63 us
  transfers between devices with their start and end apart: 20, of which 6 were waited for; matrix products, arithmetic and copies ran while one was open for 1% of the time, Pallas kernels for 23%

profile of v2, /device:TPU:0, one launch (start us, length us, event | category | flops | bytes accessed | tf_op | source)
XLA Modules:
  0.0 76.3 jit_solution(5685476327903559472)
XLA Ops:
  0.6 3.1 %collective-permute-start.1 = (bf16[16,576]{1,0:T(8,128)(2,1)}, bf16[16,576]{1,0:T(8,128)(2,1)S(1)}, u32[]{:S(2)}, u32[]{:S(2)}) collective-permute-start(bf16[16,576]{1,0:T(8,128)(2,1)} %param.13), channel_id=1, source_target_pairs={{0,8},{4,12},{8,0},{12,4},{16,24},{20,28},{24,16},{28,20},{1,9},{5... | collective-permute-start | bytes 55304 | tf_op jit(solution)/shard_map/ppermute | solution.py:454
  3.7 2.6 %collective-permute-start.2 = (bf16[16,576]{1,0:T(8,128)(2,1)}, bf16[16,576]{1,0:T(8,128)(2,1)S(1)}, u32[]{:S(2)}, u32[]{:S(2)}) collective-permute-start(bf16[16,576]{1,0:T(8,128)(2,1)} %param.13), channel_id=1, source_target_pairs={{0,16},{4,20},{8,24},{12,28},{16,0},{20,4},{24,8},{28,12},{1,17},{... | collective-permute-start | bytes 55304 | tf_op jit(solution)/shard_map/ppermute | solution.py:454
  6.3 0.0 collective-permute-start.3
  6.3 1.9 %collective-permute-start = (bf16[1,64,1792]{2,1,0:T(8,128)(2,1)}, bf16[1,64,1792]{2,1,0:T(8,128)(2,1)S(1)}, u32[]{:S(2)}, u32[]{:S(2)}) collective-permute-start(bf16[1,64,1792]{2,1,0:T(8,128)(2,1)} %bitcast.44), channel_id=1, source_target_pairs={{0,16},{4,20},{8,24},{12,28},{16,0},{20,4},{24,8},{28,12},{1,17},{... | collective-permute-start | bytes 688136 | tf_op jit(solution)/shard_map/ppermute | solution.py:454
  8.2 0.0 copy-start.7
  8.3 4.6 %pack_queries.1.q_ref = bf16[8,576,512]{2,1,0:T(8,128)(2,1)S(1)} custom-call(bf16[16,576,256]{2,1,0:T(8,128)(2,1)} %bitcast.41), custom_call_target="tpu_custom_call" | custom-call | flops 2415919104 | bytes 9437184 | tf_op jit(solution)/shard_map/pack_queries/pallas_call | solution.py:98
  12.9 0.0 copy-start
  12.9 2.2 %copy-done = bf16[8,576,512]{2,1,0:T(8,128)(2,1)} copy-done((bf16[8,576,512]{2,1,0:T(8,128)(2,1)}, bf16[8,576,512]{2,1,0:T(8,128)(2,1)S(1)}, u32[]{:S(2)}) %copy-start) | copy-done | bytes 4718616
  15.1 0.0 collective-permute-done.1
  15.1 0.0 collective-permute-done.2
  15.1 0.0 collective-permute-done.3
  15.1 0.0 copy-done.7
  15.1 1.6 %collective-permute-start.4 = (bf16[4,16,576]{2,1,0:T(8,128)(2,1)S(1)}, bf16[4,16,576]{2,1,0:T(8,128)(2,1)S(1)}, u32[]{:S(2)}, u32[]{:S(2)}) collective-permute-start(bf16[4,16,576]{2,1,0:T(8,128)(2,1)S(1)} %pad_maximum_fusion.2), channel_id=1, source_target_pairs={{0,1},{1,0},{2,3},{3,2},{4,5},{5,4},{6,7},{7,6},{8,9},{9,8},{10,11... | collective-permute-start | bytes 221192 | tf_op jit(solution)/shard_map/ppermute | solution.py:457
  16.7 1.5 %collective-permute-start.5 = (bf16[4,16,576]{2,1,0:T(8,128)(2,1)S(1)}, bf16[4,16,576]{2,1,0:T(8,128)(2,1)S(1)}, u32[]{:S(2)}, u32[]{:S(2)}) collective-permute-start(bf16[4,16,576]{2,1,0:T(8,128)(2,1)S(1)} %pad_maximum_fusion.2), channel_id=1, source_target_pairs={{0,2},{1,3},{2,0},{3,1},{4,6},{5,7},{6,4},{7,5},{8,10},{9,11},{10,... | collective-permute-start | bytes 221192 | tf_op jit(solution)/shard_map/ppermute | solution.py:457
  18.2 0.5 collective-permute-start.6
  18.7 0.0 copy-start.6
  18.7 6.1 %pack_grads.1 = (bf16[8,512,512]{2,1,0:T(8,128)(2,1)S(1)}, f32[8,1,512]{2,1,0:T(1,128)S(1)}, f32[8,4,128]{2,1,0:T(4,128)S(1)}) custom-call(bf16[4096,512]{1,0:T(8,128)(2,1)} %bitcast.42, bf16[4096,512]{1,0:T(8,128)(2,1)} %bitcast.43, f32[16,256]{1,0:T(8,128)} %bitcast.50), custom_call_target="tpu_custom_call" | custom-call | flops 2147483648 | bytes 12582912 | tf_op jit(solution)/shard_map/pack_grads/pallas_call | solution.py:180
  24.8 0.0 copy-start.3
  24.8 2.0 %copy-done.3 = bf16[8,512,512]{2,1,0:T(8,128)(2,1)} copy-done((bf16[8,512,512]{2,1,0:T(8,128)(2,1)}, bf16[8,512,512]{2,1,0:T(8,128)(2,1)S(1)}, u32[]{:S(2)}) %copy-start.3) | copy-done | bytes 4194328
  26.8 0.0 collective-permute-done.4
  26.8 0.0 collective-permute-done.5
  26.8 0.0 collective-permute-done.6
  26.8 0.1 pad_maximum_fusion.1.own_ref
  26.9 0.1 collective-permute-start.7
  26.9 0.1 pad_add_fusion.place_ref
  27.0 0.0 collective-permute-done
  27.0 0.0 copy-done.6
  27.1 1.5 %collective-permute-done.7.other_ref = bf16[16,16,576]{2,1,0:T(8,128)(2,1)S(1)} collective-permute-done((bf16[16,16,576]{2,1,0:T(8,128)(2,1)S(1)}, bf16[16,16,576]{2,1,0:T(8,128)(2,1)S(1)}, u32[]{:S(2)}, u32[]{:S(2)}) %collective-permute-start.7) | collective-permute-done | bytes 294944 | tf_op jit(solution)/shard_map/ppermute | solution.py:451
  28.6 0.0 copy-done.5
  28.6 2.3 %copy-done.1 = bf16[8,576,512]{2,1,0:T(8,128)(2,1)S(1)} copy-done((bf16[8,576,512]{2,1,0:T(8,128)(2,1)S(1)}, bf16[8,576,512]{2,1,0:T(8,128)(2,1)}, u32[]{:S(2)}) %copy-start.1) | copy-done | bytes 4718616
  30.9 2.2 %copy-done.4 = bf16[8,512,512]{2,1,0:T(8,128)(2,1)S(1)} copy-done((bf16[8,512,512]{2,1,0:T(8,128)(2,1)S(1)}, bf16[8,512,512]{2,1,0:T(8,128)(2,1)}, u32[]{:S(2)}) %copy-start.4) | copy-done | bytes 4194328
  33.1 8.9 %attend.1 = (f32[2,4,4,144,128]{4,3,2,1,0:T(8,128)S(1)}, bf16[8,512,512]{2,1,0:T(8,128)(2,1)S(1)}, bf16[512,576]{1,0:T(8,128)(2,1)S(1)}) custom-call(s32[2]{0:T(128)S(1)} %pad_add_fusion.place_ref, s32[256]{0:T(256)S(1)} %copy-done.5, bf16[16,16,576]{2,1,0:T(8,128)(2,1)S(1)} %pad_maximum_fusion.1.own_ref, ...), custom_call_target="tpu_custom_call" | custom-call | flops 9663676416 | bytes 14155776 | tf_op jit(solution)/shard_map/attend/pallas_call | solution.py:299
  42.0 0.1 slice_bitcast_fusion
  42.1 2.2 %collective-permute-start.8 = (f32[4,4,144,128]{3,2,1,0:T(8,128)S(1)}, f32[4,4,144,128]{3,2,1,0:T(8,128)S(1)}, u32[]{:S(2)}, u32[]{:S(2)}) collective-permute-start(f32[4,4,144,128]{3,2,1,0:T(8,128)S(1)} %slice_bitcast_fusion), channel_id=1, source_target_pairs={{0,4},{4,0},{8,12},{12,8},{16,20},{20,16},{24,28},{28,24},{1,5},{5... | collective-permute-start | bytes 3538952 | tf_op jit(solution)/shard_map/ppermute | solution.py:451
  44.3 2.2 %collective-permute-start.18 = (bf16[2,64,1792]{2,1,0:T(8,128)(2,1)S(1)}, bf16[2,64,1792]{2,1,0:T(8,128)(2,1)S(1)}, u32[]{:S(2)}, u32[]{:S(2)}) collective-permute-start(bf16[2,64,1792]{2,1,0:T(8,128)(2,1)S(1)} %pad_maximum_fusion), channel_id=1, source_target_pairs={{0,8},{4,12},{8,0},{12,4},{16,24},{20,28},{24,16},{28,20},{1,9},{5... | collective-permute-start | bytes 1376264 | tf_op jit(solution)/shard_map/ppermute | solution.py:454
  46.6 0.2 collective-permute-done.8
  46.8 0.2 fusion
  47.0 1.6 %collective-permute-start.10 = (bf16[4,144,128]{2,1,0:T(8,128)(2,1)S(1)}, bf16[4,144,128]{2,1,0:T(8,128)(2,1)S(1)}, u32[]{:S(2)}, u32[]{:S(2)}) collective-permute-start(bf16[4,144,128]{2,1,0:T(8,128)(2,1)S(1)} %get-tuple-element.25), channel_id=1, source_target_pairs={{0,2},{1,3},{2,0},{3,1},{4,6},{5,7},{6,4},{7,5},{8,10},{9,11},{10,... | collective-permute-start | bytes 442376 | tf_op jit(solution)/shard_map/ppermute | solution.py:457
  48.6 1.4 %collective-permute-start.11 = (bf16[4,144,128]{2,1,0:T(8,128)(2,1)S(1)}, bf16[4,144,128]{2,1,0:T(8,128)(2,1)S(1)}, u32[]{:S(2)}, u32[]{:S(2)}) collective-permute-start(bf16[4,144,128]{2,1,0:T(8,128)(2,1)S(1)} %get-tuple-element.24), channel_id=1, source_target_pairs={{0,3},{1,2},{2,1},{3,0},{4,7},{5,6},{6,5},{7,4},{8,11},{9,10},{10,... | collective-permute-start | bytes 442376 | tf_op jit(solution)/shard_map/ppermute | solution.py:457
  50.0 0.5 collective-permute-start.9
  50.6 6.7 %collective-permute-done.18 = bf16[2,64,1792]{2,1,0:T(8,128)(2,1)S(1)} collective-permute-done((bf16[2,64,1792]{2,1,0:T(8,128)(2,1)S(1)}, bf16[2,64,1792]{2,1,0:T(8,128)(2,1)S(1)}, u32[]{:S(2)}, u32[]{:S(2)}) %collective-permute-start.18) | collective-permute-done | bytes 458784 | tf_op jit(solution)/shard_map/ppermute | solution.py:454
  57.3 0.1 collective-permute-start.19
  57.4 0.0 collective-permute-done.10
  57.4 0.0 collective-permute-done.11
  57.4 0.2 collective-permute-done.9
  57.6 0.1 fusion.3
  57.7 2.3 %collective-permute-start.12 = (bf16[144,128]{1,0:T(8,128)(2,1)S(1)}, bf16[144,128]{1,0:T(8,128)(2,1)S(1)}, u32[]{:S(2)}, u32[]{:S(2)}) collective-permute-start(bf16[144,128]{1,0:T(8,128)(2,1)S(1)} %get-tuple-element.26), channel_id=1, source_target_pairs={{0,8},{4,12},{8,0},{12,4},{16,24},{20,28},{24,16},{28,20},{1,9},{5... | collective-permute-start | bytes 110600 | tf_op jit(solution)/shard_map/ppermute | solution.py:454
  60.0 0.3 collective-permute-start.13
  60.3 2.1 %collective-permute-start.14 = (bf16[144,128]{1,0:T(8,128)(2,1)S(1)}, bf16[144,128]{1,0:T(8,128)(2,1)S(1)}, u32[]{:S(2)}, u32[]{:S(2)}) collective-permute-start(bf16[144,128]{1,0:T(8,128)(2,1)S(1)} %get-tuple-element.27), channel_id=1, source_target_pairs={{0,24},{4,28},{8,16},{12,20},{16,8},{20,12},{24,0},{28,4},{1,25},{... | collective-permute-start | bytes 110600 | tf_op jit(solution)/shard_map/ppermute | solution.py:454
  62.4 2.2 %query_gradient.2.refs_0_ = bf16[16,576,256]{2,1,0:T(8,128)(2,1)} custom-call(bf16[512,576]{1,0:T(8,128)(2,1)S(1)} %get-tuple-element.17.k_ref, bf16[8,512,512]{2,1,0:T(8,128)(2,1)S(1)} %get-tuple-element.18.s_ref), custom_call_target="tpu_custom_call" | custom-call | flops 603979776 | bytes 1179648 | tf_op jit(solution)/shard_map/query_gradient/pallas_call | solution.py:351
  64.6 0.0 collective-permute-done.12
  64.6 0.6 collective-permute-done.13
  65.2 0.8 %collective-permute-done.14 = bf16[144,128]{1,0:T(8,128)(2,1)S(1)} collective-permute-done((bf16[144,128]{1,0:T(8,128)(2,1)S(1)}, bf16[144,128]{1,0:T(8,128)(2,1)S(1)}, u32[]{:S(2)}, u32[]{:S(2)}) %collective-permute-start.14) | collective-permute-done | bytes 36896 | tf_op jit(solution)/shard_map/ppermute | solution.py:454
  66.0 0.0 copy-start.2
  66.1 1.7 %collective-permute-start.15 = (bf16[144,128]{1,0:T(8,128)(2,1)S(1)}, bf16[144,128]{1,0:T(8,128)(2,1)S(1)}, u32[]{:S(2)}, u32[]{:S(2)}) collective-permute-start(bf16[144,128]{1,0:T(8,128)(2,1)S(1)} %fusion.6.refs_0_), channel_id=1, source_target_pairs={{0,1},{1,0},{2,3},{3,2},{4,5},{5,4},{6,7},{7,6},{8,9},{9,8},{10,11... | collective-permute-start | bytes 110600 | tf_op jit(solution)/shard_map/ppermute | solution.py:457
  67.7 1.5 %collective-permute-start.16 = (bf16[144,128]{1,0:T(8,128)(2,1)S(1)}, bf16[144,128]{1,0:T(8,128)(2,1)S(1)}, u32[]{:S(2)}, u32[]{:S(2)}) collective-permute-start(bf16[144,128]{1,0:T(8,128)(2,1)S(1)} %fusion.6.refs_0_), channel_id=1, source_target_pairs={{0,2},{1,3},{2,0},{3,1},{4,6},{5,7},{6,4},{7,5},{8,10},{9,11},{10,... | collective-permute-start | bytes 110600 | tf_op jit(solution)/shard_map/ppermute | solution.py:457
  69.3 0.3 collective-permute-start.17
  69.6 4.4 %query_gradient.3 = bf16[16,576,256]{2,1,0:T(8,128)(2,1)} custom-call(bf16[512,576]{1,0:T(8,128)(2,1)S(1)} %get-tuple-element.17.k_ref, bf16[8,512,512]{2,1,0:T(8,128)(2,1)S(1)} %get-tuple-element.18.s_ref, bf16[16,576,256]{2,1,0:T(8,128)(2,1)} %query_gradient.2.refs_0_), custom_call_target="tpu_custom_call", output_to_operand_aliasing={{}: (2, {})} | custom-call | flops 1811939328 | bytes 3538944 | tf_op jit(solution)/shard_map/query_gradient/pallas_call | solution.py:351
  74.1 0.0 collective-permute-done.19.refs_5_
  74.1 0.0 collective-permute-done.15.refs_1_
  74.1 0.0 collective-permute-done.16.refs_2_
  74.1 0.0 collective-permute-done.17.refs_3_
  74.1 0.0 copy-done.2
  74.1 2.2 %project.1 = (bf16[72,1792]{1,0:T(8,128)(2,1)}, bf16[64,1792]{1,0:T(8,128)(2,1)}) custom-call(s32[2]{0:T(128)S(1)} %pad_add_fusion.place_ref, bf16[144,128]{1,0:T(8,128)(2,1)S(1)} %fusion.6.refs_0_, bf16[144,128]{1,0:T(8,128)(2,1)S(1)} %collective-permute-done.15.refs_1_, bf16[144,128]{1,0:T(8,128)(2,1)S(1)} %collective-permute-done.16.refs_2_, ...), custom_call_target="tpu_custom_call" | custom-call | flops 264241152 | bytes 4128768 | tf_op jit(solution)/shard_map/project/pallas_call | solution.py:422
  (10 shorter events, 0.2 us)
Async XLA Ops:
  0.6 14.5 %collective-permute-start.1 = (bf16[16,576]{1,0:T(8,128)(2,1)}, bf16[16,576]{1,0:T(8,128)(2,1)S(1)}, u32[]{:S(2)}, u32[]{:S(2)}) collective-permute-start(bf16[16,576]{1,0:T(8,128)(2,1)} %param.13), channel_id=1, source_target_pairs={{0,8},{4,12},{8,0},{12,4},{16,24},{20,28},{24,16},{28,20},{1,9},{5... | collective-permute-start | bytes 55304 | tf_op jit(solution)/shard_map/ppermute | solution.py:454
  3.7 11.3 %collective-permute-start.2 = (bf16[16,576]{1,0:T(8,128)(2,1)}, bf16[16,576]{1,0:T(8,128)(2,1)S(1)}, u32[]{:S(2)}, u32[]{:S(2)}) collective-permute-start(bf16[16,576]{1,0:T(8,128)(2,1)} %param.13), channel_id=1, source_target_pairs={{0,16},{4,20},{8,24},{12,28},{16,0},{20,4},{24,8},{28,12},{1,17},{... | collective-permute-start | bytes 55304 | tf_op jit(solution)/shard_map/ppermute | solution.py:454
  6.3 8.8 %collective-permute-start.3 = (bf16[16,576]{1,0:T(8,128)(2,1)}, bf16[16,576]{1,0:T(8,128)(2,1)S(1)}, u32[]{:S(2)}, u32[]{:S(2)}) collective-permute-start(bf16[16,576]{1,0:T(8,128)(2,1)} %param.13), channel_id=1, source_target_pairs={{0,24},{4,28},{8,16},{12,20},{16,8},{20,12},{24,0},{28,4},{1,25},{... | collective-permute-start | bytes 55304 | tf_op jit(solution)/shard_map/ppermute | solution.py:454
  6.3 20.7 %collective-permute-start = (bf16[1,64,1792]{2,1,0:T(8,128)(2,1)}, bf16[1,64,1792]{2,1,0:T(8,128)(2,1)S(1)}, u32[]{:S(2)}, u32[]{:S(2)}) collective-permute-start(bf16[1,64,1792]{2,1,0:T(8,128)(2,1)} %bitcast.44), channel_id=1, source_target_pairs={{0,16},{4,20},{8,24},{12,28},{16,0},{20,4},{24,8},{28,12},{1,17},{... | collective-permute-start | bytes 688136 | tf_op jit(solution)/shard_map/ppermute | solution.py:454
  8.2 6.8 %copy-start.7 = (bf16[16,576]{1,0:T(8,128)(2,1)S(1)}, bf16[16,576]{1,0:T(8,128)(2,1)}, u32[]{:S(2)}) copy-start(bf16[16,576]{1,0:T(8,128)(2,1)} %param.13) | copy-start | bytes 55300
  12.9 2.2 %copy-start = (bf16[8,576,512]{2,1,0:T(8,128)(2,1)}, bf16[8,576,512]{2,1,0:T(8,128)(2,1)S(1)}, u32[]{:S(2)}) copy-start(bf16[8,576,512]{2,1,0:T(8,128)(2,1)S(1)} %pack_queries.1.q_ref) | copy-start | bytes 14155780
  15.1 11.7 %collective-permute-start.4 = (bf16[4,16,576]{2,1,0:T(8,128)(2,1)S(1)}, bf16[4,16,576]{2,1,0:T(8,128)(2,1)S(1)}, u32[]{:S(2)}, u32[]{:S(2)}) collective-permute-start(bf16[4,16,576]{2,1,0:T(8,128)(2,1)S(1)} %pad_maximum_fusion.2), channel_id=1, source_target_pairs={{0,1},{1,0},{2,3},{3,2},{4,5},{5,4},{6,7},{7,6},{8,9},{9,8},{10,11... | collective-permute-start | bytes 221192 | tf_op jit(solution)/shard_map/ppermute | solution.py:457
  16.7 10.1 %collective-permute-start.5 = (bf16[4,16,576]{2,1,0:T(8,128)(2,1)S(1)}, bf16[4,16,576]{2,1,0:T(8,128)(2,1)S(1)}, u32[]{:S(2)}, u32[]{:S(2)}) collective-permute-start(bf16[4,16,576]{2,1,0:T(8,128)(2,1)S(1)} %pad_maximum_fusion.2), channel_id=1, source_target_pairs={{0,2},{1,3},{2,0},{3,1},{4,6},{5,7},{6,4},{7,5},{8,10},{9,11},{10,... | collective-permute-start | bytes 221192 | tf_op jit(solution)/shard_map/ppermute | solution.py:457
  18.2 8.6 %collective-permute-start.6 = (bf16[4,16,576]{2,1,0:T(8,128)(2,1)S(1)}, bf16[4,16,576]{2,1,0:T(8,128)(2,1)S(1)}, u32[]{:S(2)}, u32[]{:S(2)}) collective-permute-start(bf16[4,16,576]{2,1,0:T(8,128)(2,1)S(1)} %pad_maximum_fusion.2), channel_id=1, source_target_pairs={{0,3},{1,2},{2,1},{3,0},{4,7},{5,6},{6,5},{7,4},{8,11},{9,10},{10,... | collective-permute-start | bytes 221192 | tf_op jit(solution)/shard_map/ppermute | solution.py:457
  18.7 8.3 %copy-start.6 = (bf16[64,1792]{1,0:T(8,128)(2,1)S(1)}, bf16[64,1792]{1,0:T(8,128)(2,1)}, u32[]{:S(2)}) copy-start(bf16[64,1792]{1,0:T(8,128)(2,1)} %param.14) | copy-start | bytes 688132
  18.7 9.9 %copy-start.5 = (s32[256]{0:T(256)S(1)}, s32[256]{0:T(256)}, u32[]{:S(2)}) copy-start(s32[256]{0:T(256)} %parents_ref.1) | copy-start | bytes 3076
  24.8 2.0 %copy-start.3 = (bf16[8,512,512]{2,1,0:T(8,128)(2,1)}, bf16[8,512,512]{2,1,0:T(8,128)(2,1)S(1)}, u32[]{:S(2)}) copy-start(bf16[8,512,512]{2,1,0:T(8,128)(2,1)S(1)} %get-tuple-element.14.g_ref) | copy-start | bytes 12582916
  26.9 1.7 %collective-permute-start.7 = (bf16[16,16,576]{2,1,0:T(8,128)(2,1)S(1)}, bf16[16,16,576]{2,1,0:T(8,128)(2,1)S(1)}, u32[]{:S(2)}, u32[]{:S(2)}) collective-permute-start(bf16[16,16,576]{2,1,0:T(8,128)(2,1)S(1)} %pad_maximum_fusion.1.own_ref), channel_id=1, source_target_pairs={{0,4},{4,0},{8,12},{12,8},{16,20},{20,16},{24,28},{28,24},{1,5},{5... | collective-permute-start | bytes 884744 | tf_op jit(solution)/shard_map/ppermute | solution.py:451
  28.6 2.3 %copy-start.1 = (bf16[8,576,512]{2,1,0:T(8,128)(2,1)S(1)}, bf16[8,576,512]{2,1,0:T(8,128)(2,1)}, u32[]{:S(2)}) copy-start(bf16[8,576,512]{2,1,0:T(8,128)(2,1)} %copy-done) | copy-start | bytes 14155780
  30.9 2.2 %copy-start.4 = (bf16[8,512,512]{2,1,0:T(8,128)(2,1)S(1)}, bf16[8,512,512]{2,1,0:T(8,128)(2,1)}, u32[]{:S(2)}) copy-start(bf16[8,512,512]{2,1,0:T(8,128)(2,1)} %copy-done.3) | copy-start | bytes 12582916
  42.1 4.7 %collective-permute-start.8 = (f32[4,4,144,128]{3,2,1,0:T(8,128)S(1)}, f32[4,4,144,128]{3,2,1,0:T(8,128)S(1)}, u32[]{:S(2)}, u32[]{:S(2)}) collective-permute-start(f32[4,4,144,128]{3,2,1,0:T(8,128)S(1)} %slice_bitcast_fusion), channel_id=1, source_target_pairs={{0,4},{4,0},{8,12},{12,8},{16,20},{20,16},{24,28},{28,24},{1,5},{5... | collective-permute-start | bytes 3538952 | tf_op jit(solution)/shard_map/ppermute | solution.py:451
  44.3 13.0 %collective-permute-start.18 = (bf16[2,64,1792]{2,1,0:T(8,128)(2,1)S(1)}, bf16[2,64,1792]{2,1,0:T(8,128)(2,1)S(1)}, u32[]{:S(2)}, u32[]{:S(2)}) collective-permute-start(bf16[2,64,1792]{2,1,0:T(8,128)(2,1)S(1)} %pad_maximum_fusion), channel_id=1, source_target_pairs={{0,8},{4,12},{8,0},{12,4},{16,24},{20,28},{24,16},{28,20},{1,9},{5... | collective-permute-start | bytes 1376264 | tf_op jit(solution)/shard_map/ppermute | solution.py:454
  47.0 10.4 %collective-permute-start.10 = (bf16[4,144,128]{2,1,0:T(8,128)(2,1)S(1)}, bf16[4,144,128]{2,1,0:T(8,128)(2,1)S(1)}, u32[]{:S(2)}, u32[]{:S(2)}) collective-permute-start(bf16[4,144,128]{2,1,0:T(8,128)(2,1)S(1)} %get-tuple-element.25), channel_id=1, source_target_pairs={{0,2},{1,3},{2,0},{3,1},{4,6},{5,7},{6,4},{7,5},{8,10},{9,11},{10,... | collective-permute-start | bytes 442376 | tf_op jit(solution)/shard_map/ppermute | solution.py:457
  48.6 8.8 %collective-permute-start.11 = (bf16[4,144,128]{2,1,0:T(8,128)(2,1)S(1)}, bf16[4,144,128]{2,1,0:T(8,128)(2,1)S(1)}, u32[]{:S(2)}, u32[]{:S(2)}) collective-permute-start(bf16[4,144,128]{2,1,0:T(8,128)(2,1)S(1)} %get-tuple-element.24), channel_id=1, source_target_pairs={{0,3},{1,2},{2,1},{3,0},{4,7},{5,6},{6,5},{7,4},{8,11},{9,10},{10,... | collective-permute-start | bytes 442376 | tf_op jit(solution)/shard_map/ppermute | solution.py:457
  50.0 7.6 %collective-permute-start.9 = (bf16[4,144,128]{2,1,0:T(8,128)(2,1)S(1)}, bf16[4,144,128]{2,1,0:T(8,128)(2,1)S(1)}, u32[]{:S(2)}, u32[]{:S(2)}) collective-permute-start(bf16[4,144,128]{2,1,0:T(8,128)(2,1)S(1)} %get-tuple-element.23), channel_id=1, source_target_pairs={{0,1},{1,0},{2,3},{3,2},{4,5},{5,4},{6,7},{7,6},{8,9},{9,8},{10,11... | collective-permute-start | bytes 442376 | tf_op jit(solution)/shard_map/ppermute | solution.py:457
  57.3 16.7 %collective-permute-start.19 = (bf16[4,64,1792]{2,1,0:T(8,128)(2,1)S(1)}, bf16[4,64,1792]{2,1,0:T(8,128)(2,1)S(1)}, u32[]{:S(2)}, u32[]{:S(2)}) collective-permute-start(bf16[4,64,1792]{2,1,0:T(8,128)(2,1)S(1)} %constant_dynamic-update-slice_fusion.refs_4_), channel_id=1, source_target_pairs={{0,4},{4,0},{8,12},{12,8},{16,20},{20,16},{24,28},{28,24},{1,5},{5... | collective-permute-start | bytes 2752520 | tf_op jit(solution)/shard_map/ppermute | solution.py:451
  57.7 6.9 %collective-permute-start.12 = (bf16[144,128]{1,0:T(8,128)(2,1)S(1)}, bf16[144,128]{1,0:T(8,128)(2,1)S(1)}, u32[]{:S(2)}, u32[]{:S(2)}) collective-permute-start(bf16[144,128]{1,0:T(8,128)(2,1)S(1)} %get-tuple-element.26), channel_id=1, source_target_pairs={{0,8},{4,12},{8,0},{12,4},{16,24},{20,28},{24,16},{28,20},{1,9},{5... | collective-permute-start | bytes 110600 | tf_op jit(solution)/shard_map/ppermute | solution.py:454
  60.0 5.2 %collective-permute-start.13 = (bf16[144,128]{1,0:T(8,128)(2,1)S(1)}, bf16[144,128]{1,0:T(8,128)(2,1)S(1)}, u32[]{:S(2)}, u32[]{:S(2)}) collective-permute-start(bf16[144,128]{1,0:T(8,128)(2,1)S(1)} %get-tuple-element.28), channel_id=1, source_target_pairs={{0,16},{4,20},{8,24},{12,28},{16,0},{20,4},{24,8},{28,12},{1,17},{... | collective-permute-start | bytes 110600 | tf_op jit(solution)/shard_map/ppermute | solution.py:454
  60.3 5.8 %collective-permute-start.14 = (bf16[144,128]{1,0:T(8,128)(2,1)S(1)}, bf16[144,128]{1,0:T(8,128)(2,1)S(1)}, u32[]{:S(2)}, u32[]{:S(2)}) collective-permute-start(bf16[144,128]{1,0:T(8,128)(2,1)S(1)} %get-tuple-element.27), channel_id=1, source_target_pairs={{0,24},{4,28},{8,16},{12,20},{16,8},{20,12},{24,0},{28,4},{1,25},{... | collective-permute-start | bytes 110600 | tf_op jit(solution)/shard_map/ppermute | solution.py:454
  66.0 8.1 %copy-start.2 = (bf16[576,1792]{1,0:T(8,128)(2,1)S(1)}, bf16[576,1792]{1,0:T(8,128)(2,1)}, u32[]{:S(2)}) copy-start(bf16[576,1792]{1,0:T(8,128)(2,1)} %refs_6_.1) | copy-start | bytes 6193156
  66.1 8.0 %collective-permute-start.15 = (bf16[144,128]{1,0:T(8,128)(2,1)S(1)}, bf16[144,128]{1,0:T(8,128)(2,1)S(1)}, u32[]{:S(2)}, u32[]{:S(2)}) collective-permute-start(bf16[144,128]{1,0:T(8,128)(2,1)S(1)} %fusion.6.refs_0_), channel_id=1, source_target_pairs={{0,1},{1,0},{2,3},{3,2},{4,5},{5,4},{6,7},{7,6},{8,9},{9,8},{10,11... | collective-permute-start | bytes 110600 | tf_op jit(solution)/shard_map/ppermute | solution.py:457
  67.7 6.3 %collective-permute-start.16 = (bf16[144,128]{1,0:T(8,128)(2,1)S(1)}, bf16[144,128]{1,0:T(8,128)(2,1)S(1)}, u32[]{:S(2)}, u32[]{:S(2)}) collective-permute-start(bf16[144,128]{1,0:T(8,128)(2,1)S(1)} %fusion.6.refs_0_), channel_id=1, source_target_pairs={{0,2},{1,3},{2,0},{3,1},{4,6},{5,7},{6,4},{7,5},{8,10},{9,11},{10,... | collective-permute-start | bytes 110600 | tf_op jit(solution)/shard_map/ppermute | solution.py:457
  69.3 4.9 %collective-permute-start.17 = (bf16[144,128]{1,0:T(8,128)(2,1)S(1)}, bf16[144,128]{1,0:T(8,128)(2,1)S(1)}, u32[]{:S(2)}, u32[]{:S(2)}) collective-permute-start(bf16[144,128]{1,0:T(8,128)(2,1)S(1)} %fusion.6.refs_0_), channel_id=1, source_target_pairs={{0,3},{1,2},{2,1},{3,0},{4,7},{5,6},{6,5},{7,4},{8,11},{9,10},{10,... | collective-permute-start | bytes 110600 | tf_op jit(solution)/shard_map/ppermute | solution.py:457

commit v3 on v2

--- a/solution.py
+++ b/solution.py
@@ -9,6 +9,7 @@
 LANES = 128
 GROUP = LANES // BRANCH
 KEY_TILE = 256
+COLUMN_CHUNK = 256
 
 
 softmax_scale = 192.0 ** (-0.5)
@@ -59,7 +60,7 @@
 
 def pack_queries(queries_t):
     heads, width, tokens = queries_t.shape
-    halves, groups, chunks = tokens // LANES, heads // GROUP, 6
+    halves, groups, chunks = tokens // LANES, heads // GROUP, 9
     rows = width // chunks
 
     def body(q_hbm, out_ref, q_ref, sems, perm):
@@ -220,7 +221,7 @@
     part = payload // ha
 
     def body(place_ref, parents_ref, own_ref, other_ref, q_ref, g_ref, lse_ref, delta_ref,
-             send_ref, score_ref, keys, acc_q, acc_g, pack):
+             send_ref, score_ref, keys, acc_q, acc_g, pack, prob_low):
         me_ba, me_ha = place_ref[0], place_ref[1]
         me_col, me_core = jnp.right_shift(me_ba, 1), jnp.bitwise_and(me_ba, 1)
 
@@ -248,22 +249,30 @@
                     @pl.when(wanted)
                     def _(rows=slice(start, start + size), size=size, start=start):
                         key_block = keys[rows, :]
-                        scores = jnp.dot(key_block, q_ref[b], preferred_element_type=F32) * softmax_scale
-                        at = start + lax.broadcasted_iota(jnp.int32, scores.shape, 0)
-                        prob = jnp.where(at <= limit, jnp.exp(scores - lse_row), F32(0))
-                        grad_prob = jnp.dot(key_block[:, :rank], g_ref[b], preferred_element_type=F32)
-                        grad_score = (prob * (grad_prob - delta_ref[b])).astype(BF16)
-                        score_ref[b, rows, :] = grad_score
+                        for c in range(0, cols, COLUMN_CHUNK):
+                            part_of = slice(c, c + COLUMN_CHUNK)
+                            scores = (
+                                jnp.dot(key_block, q_ref[b, :, part_of], preferred_element_type=F32)
+                                * softmax_scale
+                            )
+                            at = start + lax.broadcasted_iota(jnp.int32, scores.shape, 0)
+                            prob = jnp.where(at <= limit, jnp.exp(scores - lse_row[:, part_of]), F32(0))
+                            grad_prob = jnp.dot(
+                                key_block[:, :rank], g_ref[b, :, part_of], preferred_element_type=F32
+                            )
+                            grad_score = prob * (grad_prob - delta_ref[b, :, part_of])
+                            score_ref[b, rows, part_of] = grad_score.astype(BF16)
+                            prob_low[:size, part_of] = prob.astype(BF16)
                         if size < key_tile:
                             score_ref[b, start + size : start + key_tile, :] = jnp.zeros(
                                 (key_tile - size, cols), BF16
                             )
                         across = (((1,), (1,)), ((), ()))
                         acc_q[:, rows] += lax.dot_general(
-                            q_ref[b], grad_score, across, preferred_element_type=F32
+                            q_ref[b], score_ref[b, rows, :], across, preferred_element_type=F32
                         )
                         acc_g[:, rows] += lax.dot_general(
-                            g_ref[b], prob.astype(BF16), across, preferred_element_type=F32
+                            g_ref[b], prob_low[:size, :], across, preferred_element_type=F32
                         )
 
                 @pl.when(limit < start)
@@ -309,6 +318,7 @@
             pltpu.VMEM((width, prefix), F32),
             pltpu.VMEM((rank, prefix), F32),
             pltpu.VMEM((payload, LANES), F32),
+            pltpu.VMEM((key_tile, cols), BF16),
         ],
         compiler_params=params(24),
         cost_estimate=cost(8 * branches * cols * prefix * width, 3 * branches * cols * width * 2),

time: 76.5 us -> 76.6 us (level)
  transfers between devices with their start and end apart: 20 -> 20, of which waited for: 6 -> 5; matrix products, arithmetic and copies ran while one was open for 1% -> 1% of each run, Pallas kernels for 23% -> 23%
where the time goes in v3:
time: 76.6 us; the launch traced here: 76.4 us
  Pallas kernels  28.8 us (38%)
  starting transfers between devices  27.6 us (36%)
  waiting for transfers between devices  9.89 us (13%)
  local copies, waits for them, and re-layouts  8.86 us (12%)
  between operations  0.85 us (1%)
    ppermute x8, starting transfers between devices, over_column(): return lax.ppermute(x, 'ba', [(i, i ^ 2 * k) for i in range(ba)])  14.8 us
    ppermute x9, starting transfers between devices, over_ha(): return lax.ppermute(x, 'ha', [(i, i ^ k) for i in range(ha)])  10.7 us
    pallas_call x1, Pallas kernels, attend(): pl.pallas_call(body, in_specs=[SMEM, SMEM] + [VMEM] * 6, out_specs=[VMEM,...  8.72 us
    unnamed x17, local copies, waits for them, and re-layouts  8.71 us
    ppermute x8, waiting for transfers between devices, over_column(): return lax.ppermute(x, 'ba', [(i, i ^ 2 * k) for i in range(ba)])  8.26 us
    pallas_call x2, Pallas kernels, query_gradient(): pl.pallas_call(body, in_specs=[VMEM, VMEM] + ([] if before is None else [...  6.65 us
    pallas_call x1, Pallas kernels, pack_grads(): pl.pallas_call(body, in_specs=[HBM, HBM, HBM], out_specs=[VMEM, VMEM, VME...  6.12 us
    pallas_call x1, Pallas kernels, pack_queries(): pl.pallas_call(body, in_specs=[HBM], out_specs=VMEM, out_shape=jax.ShapeD...  5.08 us
  transfers between devices with their start and end apart: 20, of which 5 were waited for; matrix products, arithmetic and copies ran while one was open for 1% of the time, Pallas kernels for 23%

profile of v3, /device:TPU:0, one launch (start us, length us, event | category | flops | bytes accessed | tf_op | source)
XLA Modules:
  0.0 76.4 jit_solution(1058730295468771289)
XLA Ops:
  0.6 3.1 %collective-permute-start.1 = (bf16[16,576]{1,0:T(8,128)(2,1)}, bf16[16,576]{1,0:T(8,128)(2,1)S(1)}, u32[]{:S(2)}, u32[]{:S(2)}) collective-permute-start(bf16[16,576]{1,0:T(8,128)(2,1)} %param.13), channel_id=1, source_target_pairs={{0,8},{4,12},{8,0},{12,4},{16,24},{20,28},{24,16},{28,20},{1,9},{5... | collective-permute-start | bytes 55304 | tf_op jit(solution)/shard_map/ppermute | solution.py:464
  3.7 2.6 %collective-permute-start.2 = (bf16[16,576]{1,0:T(8,128)(2,1)}, bf16[16,576]{1,0:T(8,128)(2,1)S(1)}, u32[]{:S(2)}, u32[]{:S(2)}) collective-permute-start(bf16[16,576]{1,0:T(8,128)(2,1)} %param.13), channel_id=1, source_target_pairs={{0,16},{4,20},{8,24},{12,28},{16,0},{20,4},{24,8},{28,12},{1,17},{... | collective-permute-start | bytes 55304 | tf_op jit(solution)/shard_map/ppermute | solution.py:464
  6.3 0.0 collective-permute-start.3
  6.3 1.9 %collective-permute-start = (bf16[1,64,1792]{2,1,0:T(8,128)(2,1)}, bf16[1,64,1792]{2,1,0:T(8,128)(2,1)S(1)}, u32[]{:S(2)}, u32[]{:S(2)}) collective-permute-start(bf16[1,64,1792]{2,1,0:T(8,128)(2,1)} %bitcast.44), channel_id=1, source_target_pairs={{0,16},{4,20},{8,24},{12,28},{16,0},{20,4},{24,8},{28,12},{1,17},{... | collective-permute-start | bytes 688136 | tf_op jit(solution)/shard_map/ppermute | solution.py:464
  8.2 0.0 copy-start.7
  8.3 5.1 %pack_queries.1.q_ref = bf16[8,576,512]{2,1,0:T(8,128)(2,1)S(1)} custom-call(bf16[16,576,256]{2,1,0:T(8,128)(2,1)} %bitcast.41), custom_call_target="tpu_custom_call" | custom-call | flops 2415919104 | bytes 9437184 | tf_op jit(solution)/shard_map/pack_queries/pallas_call | solution.py:99
  13.3 0.0 copy-start
  13.4 2.2 %copy-done = bf16[8,576,512]{2,1,0:T(8,128)(2,1)} copy-done((bf16[8,576,512]{2,1,0:T(8,128)(2,1)}, bf16[8,576,512]{2,1,0:T(8,128)(2,1)S(1)}, u32[]{:S(2)}) %copy-start) | copy-done | bytes 4718616
  15.5 0.0 collective-permute-done.1
  15.5 0.0 collective-permute-done.2
  15.5 0.0 collective-permute-done.3
  15.5 0.0 copy-done.7
  15.6 1.6 %collective-permute-start.4 = (bf16[4,16,576]{2,1,0:T(8,128)(2,1)S(1)}, bf16[4,16,576]{2,1,0:T(8,128)(2,1)S(1)}, u32[]{:S(2)}, u32[]{:S(2)}) collective-permute-start(bf16[4,16,576]{2,1,0:T(8,128)(2,1)S(1)} %pad_maximum_fusion.2), channel_id=1, source_target_pairs={{0,1},{1,0},{2,3},{3,2},{4,5},{5,4},{6,7},{7,6},{8,9},{9,8},{10,11... | collective-permute-start | bytes 221192 | tf_op jit(solution)/shard_map/ppermute | solution.py:467
  17.1 1.5 %collective-permute-start.5 = (bf16[4,16,576]{2,1,0:T(8,128)(2,1)S(1)}, bf16[4,16,576]{2,1,0:T(8,128)(2,1)S(1)}, u32[]{:S(2)}, u32[]{:S(2)}) collective-permute-start(bf16[4,16,576]{2,1,0:T(8,128)(2,1)S(1)} %pad_maximum_fusion.2), channel_id=1, source_target_pairs={{0,2},{1,3},{2,0},{3,1},{4,6},{5,7},{6,4},{7,5},{8,10},{9,11},{10,... | collective-permute-start | bytes 221192 | tf_op jit(solution)/shard_map/ppermute | solution.py:467
  18.7 0.5 collective-permute-start.6
  19.1 0.0 copy-start.6
  19.1 6.1 %pack_grads.1 = (bf16[8,512,512]{2,1,0:T(8,128)(2,1)S(1)}, f32[8,1,512]{2,1,0:T(1,128)S(1)}, f32[8,4,128]{2,1,0:T(4,128)S(1)}) custom-call(bf16[4096,512]{1,0:T(8,128)(2,1)} %bitcast.42, bf16[4096,512]{1,0:T(8,128)(2,1)} %bitcast.43, f32[16,256]{1,0:T(8,128)} %bitcast.50), custom_call_target="tpu_custom_call" | custom-call | flops 2147483648 | bytes 12582912 | tf_op jit(solution)/shard_map/pack_grads/pallas_call | solution.py:181
  25.3 0.0 copy-start.3
  25.3 2.0 %copy-done.3 = bf16[8,512,512]{2,1,0:T(8,128)(2,1)} copy-done((bf16[8,512,512]{2,1,0:T(8,128)(2,1)}, bf16[8,512,512]{2,1,0:T(8,128)(2,1)S(1)}, u32[]{:S(2)}) %copy-start.3) | copy-done | bytes 4194328
  27.2 0.0 collective-permute-done.4
  27.2 0.0 collective-permute-done.5
  27.2 0.0 collective-permute-done.6
  27.2 0.1 pad_maximum_fusion.1.own_ref
  27.3 0.1 collective-permute-start.7
  27.4 0.1 pad_add_fusion.place_ref
  27.5 0.0 collective-permute-done
  27.5 0.0 copy-done.6
  27.5 1.5 %collective-permute-done.7.other_ref = bf16[16,16,576]{2,1,0:T(8,128)(2,1)S(1)} collective-permute-done((bf16[16,16,576]{2,1,0:T(8,128)(2,1)S(1)}, bf16[16,16,576]{2,1,0:T(8,128)(2,1)S(1)}, u32[]{:S(2)}, u32[]{:S(2)}) %collective-permute-start.7) | collective-permute-done | bytes 294944 | tf_op jit(solution)/shard_map/ppermute | solution.py:461
  29.0 0.0 copy-done.5
  29.0 2.3 %copy-done.1 = bf16[8,576,512]{2,1,0:T(8,128)(2,1)S(1)} copy-done((bf16[8,576,512]{2,1,0:T(8,128)(2,1)S(1)}, bf16[8,576,512]{2,1,0:T(8,128)(2,1)}, u32[]{:S(2)}) %copy-start.1) | copy-done | bytes 4718616
  31.4 2.2 %copy-done.4 = bf16[8,512,512]{2,1,0:T(8,128)(2,1)S(1)} copy-done((bf16[8,512,512]{2,1,0:T(8,128)(2,1)S(1)}, bf16[8,512,512]{2,1,0:T(8,128)(2,1)}, u32[]{:S(2)}) %copy-start.4) | copy-done | bytes 4194328
  33.5 8.7 %attend.1 = (f32[2,4,4,144,128]{4,3,2,1,0:T(8,128)S(1)}, bf16[8,512,512]{2,1,0:T(8,128)(2,1)S(1)}, bf16[512,576]{1,0:T(8,128)(2,1)S(1)}) custom-call(s32[2]{0:T(128)S(1)} %pad_add_fusion.place_ref, s32[256]{0:T(256)S(1)} %copy-done.5, bf16[16,16,576]{2,1,0:T(8,128)(2,1)S(1)} %pad_maximum_fusion.1.own_ref, ...), custom_call_target="tpu_custom_call" | custom-call | flops 9663676416 | bytes 14155776 | tf_op jit(solution)/shard_map/attend/pallas_call | solution.py:308
  42.3 0.1 slice_bitcast_fusion
  42.4 1.9 %collective-permute-start.8 = (f32[4,4,144,128]{3,2,1,0:T(8,128)S(1)}, f32[4,4,144,128]{3,2,1,0:T(8,128)S(1)}, u32[]{:S(2)}, u32[]{:S(2)}) collective-permute-start(f32[4,4,144,128]{3,2,1,0:T(8,128)S(1)} %slice_bitcast_fusion), channel_id=1, source_target_pairs={{0,4},{4,0},{8,12},{12,8},{16,20},{20,16},{24,28},{28,24},{1,5},{5... | collective-permute-start | bytes 3538952 | tf_op jit(solution)/shard_map/ppermute | solution.py:461
  44.3 2.4 %collective-permute-start.18 = (bf16[2,64,1792]{2,1,0:T(8,128)(2,1)S(1)}, bf16[2,64,1792]{2,1,0:T(8,128)(2,1)S(1)}, u32[]{:S(2)}, u32[]{:S(2)}) collective-permute-start(bf16[2,64,1792]{2,1,0:T(8,128)(2,1)S(1)} %pad_maximum_fusion), channel_id=1, source_target_pairs={{0,8},{4,12},{8,0},{12,4},{16,24},{20,28},{24,16},{28,20},{1,9},{5... | collective-permute-start | bytes 1376264 | tf_op jit(solution)/shard_map/ppermute | solution.py:464
  46.7 0.1 collective-permute-done.8
  46.8 0.2 fusion
  47.0 1.6 %collective-permute-start.10 = (bf16[4,144,128]{2,1,0:T(8,128)(2,1)S(1)}, bf16[4,144,128]{2,1,0:T(8,128)(2,1)S(1)}, u32[]{:S(2)}, u32[]{:S(2)}) collective-permute-start(bf16[4,144,128]{2,1,0:T(8,128)(2,1)S(1)} %get-tuple-element.25), channel_id=1, source_target_pairs={{0,2},{1,3},{2,0},{3,1},{4,6},{5,7},{6,4},{7,5},{8,10},{9,11},{10,... | collective-permute-start | bytes 442376 | tf_op jit(solution)/shard_map/ppermute | solution.py:467
  48.6 1.4 %collective-permute-start.11 = (bf16[4,144,128]{2,1,0:T(8,128)(2,1)S(1)}, bf16[4,144,128]{2,1,0:T(8,128)(2,1)S(1)}, u32[]{:S(2)}, u32[]{:S(2)}) collective-permute-start(bf16[4,144,128]{2,1,0:T(8,128)(2,1)S(1)} %get-tuple-element.24), channel_id=1, source_target_pairs={{0,3},{1,2},{2,1},{3,0},{4,7},{5,6},{6,5},{7,4},{8,11},{9,10},{10,... | collective-permute-start | bytes 442376 | tf_op jit(solution)/shard_map/ppermute | solution.py:467
  50.0 0.5 collective-permute-start.9
  50.5 6.9 %collective-permute-done.18 = bf16[2,64,1792]{2,1,0:T(8,128)(2,1)S(1)} collective-permute-done((bf16[2,64,1792]{2,1,0:T(8,128)(2,1)S(1)}, bf16[2,64,1792]{2,1,0:T(8,128)(2,1)S(1)}, u32[]{:S(2)}, u32[]{:S(2)}) %collective-permute-start.18) | collective-permute-done | bytes 458784 | tf_op jit(solution)/shard_map/ppermute | solution.py:464
  57.5 0.1 collective-permute-start.19
  57.5 0.0 collective-permute-done.10
  57.5 0.0 collective-permute-done.11
  57.6 0.0 collective-permute-done.9
  57.6 0.1 fusion.3
  57.7 2.4 %collective-permute-start.12 = (bf16[144,128]{1,0:T(8,128)(2,1)S(1)}, bf16[144,128]{1,0:T(8,128)(2,1)S(1)}, u32[]{:S(2)}, u32[]{:S(2)}) collective-permute-start(bf16[144,128]{1,0:T(8,128)(2,1)S(1)} %get-tuple-element.26), channel_id=1, source_target_pairs={{0,8},{4,12},{8,0},{12,4},{16,24},{20,28},{24,16},{28,20},{1,9},{5... | collective-permute-start | bytes 110600 | tf_op jit(solution)/shard_map/ppermute | solution.py:464
  60.1 0.3 collective-permute-start.13
  60.3 2.2 %collective-permute-start.14 = (bf16[144,128]{1,0:T(8,128)(2,1)S(1)}, bf16[144,128]{1,0:T(8,128)(2,1)S(1)}, u32[]{:S(2)}, u32[]{:S(2)}) collective-permute-start(bf16[144,128]{1,0:T(8,128)(2,1)S(1)} %get-tuple-element.27), channel_id=1, source_target_pairs={{0,24},{4,28},{8,16},{12,20},{16,8},{20,12},{24,0},{28,4},{1,25},{... | collective-permute-start | bytes 110600 | tf_op jit(solution)/shard_map/ppermute | solution.py:464
  62.5 2.2 %query_gradient.2.refs_0_ = bf16[16,576,256]{2,1,0:T(8,128)(2,1)} custom-call(bf16[512,576]{1,0:T(8,128)(2,1)S(1)} %get-tuple-element.17.k_ref, bf16[8,512,512]{2,1,0:T(8,128)(2,1)S(1)} %get-tuple-element.18.s_ref), custom_call_target="tpu_custom_call" | custom-call | flops 603979776 | bytes 1179648 | tf_op jit(solution)/shard_map/query_gradient/pallas_call | solution.py:361
  64.7 0.0 collective-permute-done.12
  64.8 0.6 collective-permute-done.13
  65.3 0.8 %collective-permute-done.14 = bf16[144,128]{1,0:T(8,128)(2,1)S(1)} collective-permute-done((bf16[144,128]{1,0:T(8,128)(2,1)S(1)}, bf16[144,128]{1,0:T(8,128)(2,1)S(1)}, u32[]{:S(2)}, u32[]{:S(2)}) %collective-permute-start.14) | collective-permute-done | bytes 36896 | tf_op jit(solution)/shard_map/ppermute | solution.py:464
  66.2 0.0 copy-start.2
  66.2 1.7 %collective-permute-start.15 = (bf16[144,128]{1,0:T(8,128)(2,1)S(1)}, bf16[144,128]{1,0:T(8,128)(2,1)S(1)}, u32[]{:S(2)}, u32[]{:S(2)}) collective-permute-start(bf16[144,128]{1,0:T(8,128)(2,1)S(1)} %fusion.6.refs_0_), channel_id=1, source_target_pairs={{0,1},{1,0},{2,3},{3,2},{4,5},{5,4},{6,7},{7,6},{8,9},{9,8},{10,11... | collective-permute-start | bytes 110600 | tf_op jit(solution)/shard_map/ppermute | solution.py:467
  67.8 1.5 %collective-permute-start.16 = (bf16[144,128]{1,0:T(8,128)(2,1)S(1)}, bf16[144,128]{1,0:T(8,128)(2,1)S(1)}, u32[]{:S(2)}, u32[]{:S(2)}) collective-permute-start(bf16[144,128]{1,0:T(8,128)(2,1)S(1)} %fusion.6.refs_0_), channel_id=1, source_target_pairs={{0,2},{1,3},{2,0},{3,1},{4,6},{5,7},{6,4},{7,5},{8,10},{9,11},{10,... | collective-permute-start | bytes 110600 | tf_op jit(solution)/shard_map/ppermute | solution.py:467
  69.4 0.4 collective-permute-start.17
  69.7 4.4 %query_gradient.3 = bf16[16,576,256]{2,1,0:T(8,128)(2,1)} custom-call(bf16[512,576]{1,0:T(8,128)(2,1)S(1)} %get-tuple-element.17.k_ref, bf16[8,512,512]{2,1,0:T(8,128)(2,1)S(1)} %get-tuple-element.18.s_ref, bf16[16,576,256]{2,1,0:T(8,128)(2,1)} %query_gradient.2.refs_0_), custom_call_target="tpu_custom_call", output_to_operand_aliasing={{}: (2, {})} | custom-call | flops 1811939328 | bytes 3538944 | tf_op jit(solution)/shard_map/query_gradient/pallas_call | solution.py:361
  74.2 0.0 collective-permute-done.19.refs_5_
  74.2 0.0 collective-permute-done.15.refs_1_
  74.2 0.0 collective-permute-done.16.refs_2_
  74.2 0.0 collective-permute-done.17.refs_3_
  74.2 0.0 copy-done.2
  74.2 2.2 %project.1 = (bf16[72,1792]{1,0:T(8,128)(2,1)}, bf16[64,1792]{1,0:T(8,128)(2,1)}) custom-call(s32[2]{0:T(128)S(1)} %pad_add_fusion.place_ref, bf16[144,128]{1,0:T(8,128)(2,1)S(1)} %fusion.6.refs_0_, bf16[144,128]{1,0:T(8,128)(2,1)S(1)} %collective-permute-done.15.refs_1_, bf16[144,128]{1,0:T(8,128)(2,1)S(1)} %collective-permute-done.16.refs_2_, ...), custom_call_target="tpu_custom_call" | custom-call | flops 264241152 | bytes 4128768 | tf_op jit(solution)/shard_map/project/pallas_call | solution.py:432
  (10 shorter events, 0.2 us)
Async XLA Ops:
  0.6 14.9 %collective-permute-start.1 = (bf16[16,576]{1,0:T(8,128)(2,1)}, bf16[16,576]{1,0:T(8,128)(2,1)S(1)}, u32[]{:S(2)}, u32[]{:S(2)}) collective-permute-start(bf16[16,576]{1,0:T(8,128)(2,1)} %param.13), channel_id=1, source_target_pairs={{0,8},{4,12},{8,0},{12,4},{16,24},{20,28},{24,16},{28,20},{1,9},{5... | collective-permute-start | bytes 55304 | tf_op jit(solution)/shard_map/ppermute | solution.py:464
  3.7 11.8 %collective-permute-start.2 = (bf16[16,576]{1,0:T(8,128)(2,1)}, bf16[16,576]{1,0:T(8,128)(2,1)S(1)}, u32[]{:S(2)}, u32[]{:S(2)}) collective-permute-start(bf16[16,576]{1,0:T(8,128)(2,1)} %param.13), channel_id=1, source_target_pairs={{0,16},{4,20},{8,24},{12,28},{16,0},{20,4},{24,8},{28,12},{1,17},{... | collective-permute-start | bytes 55304 | tf_op jit(solution)/shard_map/ppermute | solution.py:464
  6.3 9.2 %collective-permute-start.3 = (bf16[16,576]{1,0:T(8,128)(2,1)}, bf16[16,576]{1,0:T(8,128)(2,1)S(1)}, u32[]{:S(2)}, u32[]{:S(2)}) collective-permute-start(bf16[16,576]{1,0:T(8,128)(2,1)} %param.13), channel_id=1, source_target_pairs={{0,24},{4,28},{8,16},{12,20},{16,8},{20,12},{24,0},{28,4},{1,25},{... | collective-permute-start | bytes 55304 | tf_op jit(solution)/shard_map/ppermute | solution.py:464
  6.3 21.1 %collective-permute-start = (bf16[1,64,1792]{2,1,0:T(8,128)(2,1)}, bf16[1,64,1792]{2,1,0:T(8,128)(2,1)S(1)}, u32[]{:S(2)}, u32[]{:S(2)}) collective-permute-start(bf16[1,64,1792]{2,1,0:T(8,128)(2,1)} %bitcast.44), channel_id=1, source_target_pairs={{0,16},{4,20},{8,24},{12,28},{16,0},{20,4},{24,8},{28,12},{1,17},{... | collective-permute-start | bytes 688136 | tf_op jit(solution)/shard_map/ppermute | solution.py:464
  8.2 7.3 %copy-start.7 = (bf16[16,576]{1,0:T(8,128)(2,1)S(1)}, bf16[16,576]{1,0:T(8,128)(2,1)}, u32[]{:S(2)}) copy-start(bf16[16,576]{1,0:T(8,128)(2,1)} %param.13) | copy-start | bytes 55300
  13.3 2.2 %copy-start = (bf16[8,576,512]{2,1,0:T(8,128)(2,1)}, bf16[8,576,512]{2,1,0:T(8,128)(2,1)S(1)}, u32[]{:S(2)}) copy-start(bf16[8,576,512]{2,1,0:T(8,128)(2,1)S(1)} %pack_queries.1.q_ref) | copy-start | bytes 14155780
  15.6 11.7 %collective-permute-start.4 = (bf16[4,16,576]{2,1,0:T(8,128)(2,1)S(1)}, bf16[4,16,576]{2,1,0:T(8,128)(2,1)S(1)}, u32[]{:S(2)}, u32[]{:S(2)}) collective-permute-start(bf16[4,16,576]{2,1,0:T(8,128)(2,1)S(1)} %pad_maximum_fusion.2), channel_id=1, source_target_pairs={{0,1},{1,0},{2,3},{3,2},{4,5},{5,4},{6,7},{7,6},{8,9},{9,8},{10,11... | collective-permute-start | bytes 221192 | tf_op jit(solution)/shard_map/ppermute | solution.py:467
  17.1 10.1 %collective-permute-start.5 = (bf16[4,16,576]{2,1,0:T(8,128)(2,1)S(1)}, bf16[4,16,576]{2,1,0:T(8,128)(2,1)S(1)}, u32[]{:S(2)}, u32[]{:S(2)}) collective-permute-start(bf16[4,16,576]{2,1,0:T(8,128)(2,1)S(1)} %pad_maximum_fusion.2), channel_id=1, source_target_pairs={{0,2},{1,3},{2,0},{3,1},{4,6},{5,7},{6,4},{7,5},{8,10},{9,11},{10,... | collective-permute-start | bytes 221192 | tf_op jit(solution)/shard_map/ppermute | solution.py:467
  18.7 8.6 %collective-permute-start.6 = (bf16[4,16,576]{2,1,0:T(8,128)(2,1)S(1)}, bf16[4,16,576]{2,1,0:T(8,128)(2,1)S(1)}, u32[]{:S(2)}, u32[]{:S(2)}) collective-permute-start(bf16[4,16,576]{2,1,0:T(8,128)(2,1)S(1)} %pad_maximum_fusion.2), channel_id=1, source_target_pairs={{0,3},{1,2},{2,1},{3,0},{4,7},{5,6},{6,5},{7,4},{8,11},{9,10},{10,... | collective-permute-start | bytes 221192 | tf_op jit(solution)/shard_map/ppermute | solution.py:467
  19.1 8.3 %copy-start.6 = (bf16[64,1792]{1,0:T(8,128)(2,1)S(1)}, bf16[64,1792]{1,0:T(8,128)(2,1)}, u32[]{:S(2)}) copy-start(bf16[64,1792]{1,0:T(8,128)(2,1)} %param.14) | copy-start | bytes 688132
  19.1 9.9 %copy-start.5 = (s32[256]{0:T(256)S(1)}, s32[256]{0:T(256)}, u32[]{:S(2)}) copy-start(s32[256]{0:T(256)} %parents_ref.1) | copy-start | bytes 3076
  25.3 2.0 %copy-start.3 = (bf16[8,512,512]{2,1,0:T(8,128)(2,1)}, bf16[8,512,512]{2,1,0:T(8,128)(2,1)S(1)}, u32[]{:S(2)}) copy-start(bf16[8,512,512]{2,1,0:T(8,128)(2,1)S(1)} %get-tuple-element.14.g_ref) | copy-start | bytes 12582916
  27.3 1.7 %collective-permute-start.7 = (bf16[16,16,576]{2,1,0:T(8,128)(2,1)S(1)}, bf16[16,16,576]{2,1,0:T(8,128)(2,1)S(1)}, u32[]{:S(2)}, u32[]{:S(2)}) collective-permute-start(bf16[16,16,576]{2,1,0:T(8,128)(2,1)S(1)} %pad_maximum_fusion.1.own_ref), channel_id=1, source_target_pairs={{0,4},{4,0},{8,12},{12,8},{16,20},{20,16},{24,28},{28,24},{1,5},{5... | collective-permute-start | bytes 884744 | tf_op jit(solution)/shard_map/ppermute | solution.py:461
  29.0 2.3 %copy-start.1 = (bf16[8,576,512]{2,1,0:T(8,128)(2,1)S(1)}, bf16[8,576,512]{2,1,0:T(8,128)(2,1)}, u32[]{:S(2)}) copy-start(bf16[8,576,512]{2,1,0:T(8,128)(2,1)} %copy-done) | copy-start | bytes 14155780
  31.4 2.2 %copy-start.4 = (bf16[8,512,512]{2,1,0:T(8,128)(2,1)S(1)}, bf16[8,512,512]{2,1,0:T(8,128)(2,1)}, u32[]{:S(2)}) copy-start(bf16[8,512,512]{2,1,0:T(8,128)(2,1)} %copy-done.3) | copy-start | bytes 12582916
  42.4 4.4 %collective-permute-start.8 = (f32[4,4,144,128]{3,2,1,0:T(8,128)S(1)}, f32[4,4,144,128]{3,2,1,0:T(8,128)S(1)}, u32[]{:S(2)}, u32[]{:S(2)}) collective-permute-start(f32[4,4,144,128]{3,2,1,0:T(8,128)S(1)} %slice_bitcast_fusion), channel_id=1, source_target_pairs={{0,4},{4,0},{8,12},{12,8},{16,20},{20,16},{24,28},{28,24},{1,5},{5... | collective-permute-start | bytes 3538952 | tf_op jit(solution)/shard_map/ppermute | solution.py:461
  44.3 13.1 %collective-permute-start.18 = (bf16[2,64,1792]{2,1,0:T(8,128)(2,1)S(1)}, bf16[2,64,1792]{2,1,0:T(8,128)(2,1)S(1)}, u32[]{:S(2)}, u32[]{:S(2)}) collective-permute-start(bf16[2,64,1792]{2,1,0:T(8,128)(2,1)S(1)} %pad_maximum_fusion), channel_id=1, source_target_pairs={{0,8},{4,12},{8,0},{12,4},{16,24},{20,28},{24,16},{28,20},{1,9},{5... | collective-permute-start | bytes 1376264 | tf_op jit(solution)/shard_map/ppermute | solution.py:464
  47.0 10.6 %collective-permute-start.10 = (bf16[4,144,128]{2,1,0:T(8,128)(2,1)S(1)}, bf16[4,144,128]{2,1,0:T(8,128)(2,1)S(1)}, u32[]{:S(2)}, u32[]{:S(2)}) collective-permute-start(bf16[4,144,128]{2,1,0:T(8,128)(2,1)S(1)} %get-tuple-element.25), channel_id=1, source_target_pairs={{0,2},{1,3},{2,0},{3,1},{4,6},{5,7},{6,4},{7,5},{8,10},{9,11},{10,... | collective-permute-start | bytes 442376 | tf_op jit(solution)/shard_map/ppermute | solution.py:467
  48.6 9.0 %collective-permute-start.11 = (bf16[4,144,128]{2,1,0:T(8,128)(2,1)S(1)}, bf16[4,144,128]{2,1,0:T(8,128)(2,1)S(1)}, u32[]{:S(2)}, u32[]{:S(2)}) collective-permute-start(bf16[4,144,128]{2,1,0:T(8,128)(2,1)S(1)} %get-tuple-element.24), channel_id=1, source_target_pairs={{0,3},{1,2},{2,1},{3,0},{4,7},{5,6},{6,5},{7,4},{8,11},{9,10},{10,... | collective-permute-start | bytes 442376 | tf_op jit(solution)/shard_map/ppermute | solution.py:467
  50.0 7.6 %collective-permute-start.9 = (bf16[4,144,128]{2,1,0:T(8,128)(2,1)S(1)}, bf16[4,144,128]{2,1,0:T(8,128)(2,1)S(1)}, u32[]{:S(2)}, u32[]{:S(2)}) collective-permute-start(bf16[4,144,128]{2,1,0:T(8,128)(2,1)S(1)} %get-tuple-element.23), channel_id=1, source_target_pairs={{0,1},{1,0},{2,3},{3,2},{4,5},{5,4},{6,7},{7,6},{8,9},{9,8},{10,11... | collective-permute-start | bytes 442376 | tf_op jit(solution)/shard_map/ppermute | solution.py:467
  57.5 16.7 %collective-permute-start.19 = (bf16[4,64,1792]{2,1,0:T(8,128)(2,1)S(1)}, bf16[4,64,1792]{2,1,0:T(8,128)(2,1)S(1)}, u32[]{:S(2)}, u32[]{:S(2)}) collective-permute-start(bf16[4,64,1792]{2,1,0:T(8,128)(2,1)S(1)} %constant_dynamic-update-slice_fusion.refs_4_), channel_id=1, source_target_pairs={{0,4},{4,0},{8,12},{12,8},{16,20},{20,16},{24,28},{28,24},{1,5},{5... | collective-permute-start | bytes 2752520 | tf_op jit(solution)/shard_map/ppermute | solution.py:461
  57.7 7.1 %collective-permute-start.12 = (bf16[144,128]{1,0:T(8,128)(2,1)S(1)}, bf16[144,128]{1,0:T(8,128)(2,1)S(1)}, u32[]{:S(2)}, u32[]{:S(2)}) collective-permute-start(bf16[144,128]{1,0:T(8,128)(2,1)S(1)} %get-tuple-element.26), channel_id=1, source_target_pairs={{0,8},{4,12},{8,0},{12,4},{16,24},{20,28},{24,16},{28,20},{1,9},{5... | collective-permute-start | bytes 110600 | tf_op jit(solution)/shard_map/ppermute | solution.py:464
  60.1 5.2 %collective-permute-start.13 = (bf16[144,128]{1,0:T(8,128)(2,1)S(1)}, bf16[144,128]{1,0:T(8,128)(2,1)S(1)}, u32[]{:S(2)}, u32[]{:S(2)}) collective-permute-start(bf16[144,128]{1,0:T(8,128)(2,1)S(1)} %get-tuple-element.28), channel_id=1, source_target_pairs={{0,16},{4,20},{8,24},{12,28},{16,0},{20,4},{24,8},{28,12},{1,17},{... | collective-permute-start | bytes 110600 | tf_op jit(solution)/shard_map/ppermute | solution.py:464
  60.3 5.8 %collective-permute-start.14 = (bf16[144,128]{1,0:T(8,128)(2,1)S(1)}, bf16[144,128]{1,0:T(8,128)(2,1)S(1)}, u32[]{:S(2)}, u32[]{:S(2)}) collective-permute-start(bf16[144,128]{1,0:T(8,128)(2,1)S(1)} %get-tuple-element.27), channel_id=1, source_target_pairs={{0,24},{4,28},{8,16},{12,20},{16,8},{20,12},{24,0},{28,4},{1,25},{... | collective-permute-start | bytes 110600 | tf_op jit(solution)/shard_map/ppermute | solution.py:464
  66.2 8.1 %copy-start.2 = (bf16[576,1792]{1,0:T(8,128)(2,1)S(1)}, bf16[576,1792]{1,0:T(8,128)(2,1)}, u32[]{:S(2)}) copy-start(bf16[576,1792]{1,0:T(8,128)(2,1)} %refs_6_.1) | copy-start | bytes 6193156
  66.2 8.0 %collective-permute-start.15 = (bf16[144,128]{1,0:T(8,128)(2,1)S(1)}, bf16[144,128]{1,0:T(8,128)(2,1)S(1)}, u32[]{:S(2)}, u32[]{:S(2)}) collective-permute-start(bf16[144,128]{1,0:T(8,128)(2,1)S(1)} %fusion.6.refs_0_), channel_id=1, source_target_pairs={{0,1},{1,0},{2,3},{3,2},{4,5},{5,4},{6,7},{7,6},{8,9},{9,8},{10,11... | collective-permute-start | bytes 110600 | tf_op jit(solution)/shard_map/ppermute | solution.py:467
  67.8 6.3 %collective-permute-start.16 = (bf16[144,128]{1,0:T(8,128)(2,1)S(1)}, bf16[144,128]{1,0:T(8,128)(2,1)S(1)}, u32[]{:S(2)}, u32[]{:S(2)}) collective-permute-start(bf16[144,128]{1,0:T(8,128)(2,1)S(1)} %fusion.6.refs_0_), channel_id=1, source_target_pairs={{0,2},{1,3},{2,0},{3,1},{4,6},{5,7},{6,4},{7,5},{8,10},{9,11},{10,... | collective-permute-start | bytes 110600 | tf_op jit(solution)/shard_map/ppermute | solution.py:467
  69.4 4.9 %collective-permute-start.17 = (bf16[144,128]{1,0:T(8,128)(2,1)S(1)}, bf16[144,128]{1,0:T(8,128)(2,1)S(1)}, u32[]{:S(2)}, u32[]{:S(2)}) collective-permute-start(bf16[144,128]{1,0:T(8,128)(2,1)S(1)} %fusion.6.refs_0_), channel_id=1, source_target_pairs={{0,3},{1,2},{2,1},{3,0},{4,7},{5,6},{6,5},{7,4},{8,11},{9,10},{10,... | collective-permute-start | bytes 110600 | tf_op jit(solution)/shard_map/ppermute | solution.py:467
